TPU v7x, 8 devices: a whole 2x2x1 slice. The times are simulated.
8 devices in a mesh: data: 2 (over z, y), seq: 4 (over x, core).
Axes of the slice: x: 2, y: 2, z: 1, core: 2. Of those that a mesh axis runs over, the one named last changes fastest.
Arguments:
- act_in: bfloat16 [128, 576, 768], P('data', 'seq'), parts along dimension 0
- grad_out: bfloat16 [128, 576, 768], P('data', 'seq'), parts along dimension 0
- ln1_scale: float32 [768], replicated
- ln1_shift: float32 [768], replicated
- w_tok1: bfloat16 [576, 384], replicated
- b_tok1: float32 [384], replicated
- w_tok2: bfloat16 [384, 576], replicated
- b_tok2: float32 [576], replicated
- ln2_scale: float32 [768], replicated
- ln2_shift: float32 [768], replicated
- w_chan1: bfloat16 [768, 3072], replicated
- b_chan1: float32 [3072], replicated
- w_chan2: bfloat16 [3072, 768], replicated
- b_chan2: float32 [768], replicated
Outputs:
- output 1: bfloat16 [128, 576, 768], P('data', 'seq'), parts along dimension 0
- output 2: bfloat16 [128, 576, 768], P('data', 'seq'), parts along dimension 0
- output 3: float32 [1152, 384], P('data'), parts along dimension 0
- output 4: float32 [768, 576], P('data'), parts along dimension 0
- output 5: float32 [1536, 3072], P('data'), parts along dimension 0
- output 6: float32 [6144, 768], P('data'), parts along dimension 0
There are 2 independent parts. A program takes and returns all parts, laid end to end along the dimension named above; an argument that names none is the same for every part.
All inputs are finite; a program needn't handle non-finite values.
Results may differ from a plain program's by a relative error of at most 0.0166067.
Values are sent between devices in bfloat16 or wider.
A program may use at most 1 GiB of HBM per device.

v0:
```python
import jax
import jax.numpy as jnp
from jax import lax
from jax.sharding import PartitionSpec as P

LN_EPS = 1e-6


def layer_norm(rows_in, ln_scale, ln_shift):
    widened = rows_in.astype(jnp.float32)
    row_mean = jnp.mean(widened, axis=-1, keepdims=True)
    centered = widened - row_mean
    row_var = jnp.mean(centered * centered, axis=-1, keepdims=True)
    return (centered * lax.rsqrt(row_var + LN_EPS) * ln_scale + ln_shift).astype(jnp.bfloat16)


def gelu_bf16(pre_act):
    return jax.nn.gelu(pre_act.astype(jnp.float32)).astype(jnp.bfloat16)


def solution(mesh):
    act_spec = P("data", "seq", None)
    part_spec = P("data", None)
    spec_in = (act_spec, act_spec) + (P(),) * 12
    spec_out = (act_spec, act_spec, part_spec, part_spec, part_spec, part_spec)

    def device_step(act_loc, grad_loc, ln1_scale, ln1_shift, w_tok1, b_tok1, w_tok2, b_tok2,
                    ln2_scale, ln2_shift, w_chan1, b_chan1, w_chan2, b_chan2):
        normed, ln1_pull = jax.vjp(lambda rows_in: layer_norm(rows_in, ln1_scale, ln1_shift), act_loc)
        normed_cols = lax.all_to_all(normed, "seq", 2, 1, tiled=True)
        tok_pre = (jnp.einsum("bsc,sd->bdc", normed_cols, w_tok1, preferred_element_type=jnp.float32)
                   + b_tok1[:, None]).astype(jnp.bfloat16)
        tok_act, tok_pull = jax.vjp(gelu_bf16, tok_pre)
        tok_cols = (jnp.einsum("bdc,ds->bsc", tok_act, w_tok2, preferred_element_type=jnp.float32)
                    + b_tok2[:, None]).astype(jnp.bfloat16)
        tok_rows = lax.all_to_all(tok_cols, "seq", 1, 2, tiled=True)
        mid_act = (act_loc.astype(jnp.float32) + tok_rows.astype(jnp.float32)).astype(jnp.bfloat16)
        normed_mid, ln2_pull = jax.vjp(lambda rows_in: layer_norm(rows_in, ln2_scale, ln2_shift), mid_act)
        chan_pre = (jnp.einsum("bsc,ch->bsh", normed_mid, w_chan1, preferred_element_type=jnp.float32)
                    + b_chan1).astype(jnp.bfloat16)
        chan_act, chan_pull = jax.vjp(gelu_bf16, chan_pre)
        chan_out = jnp.einsum("bsh,hc->bsc", chan_act, w_chan2, preferred_element_type=jnp.float32) + b_chan2
        act_out = (mid_act.astype(jnp.float32) + chan_out).astype(jnp.bfloat16)

        grad_wchan2 = jnp.einsum("bsh,bsc->hc", chan_act, grad_loc, preferred_element_type=jnp.float32)
        grad_chan_act = jnp.einsum("bsc,hc->bsh", grad_loc, w_chan2,
                                   preferred_element_type=jnp.float32).astype(jnp.bfloat16)
        (grad_chan_pre,) = chan_pull(grad_chan_act)
        grad_wchan1 = jnp.einsum("bsc,bsh->ch", normed_mid, grad_chan_pre, preferred_element_type=jnp.float32)
        grad_normed_mid = jnp.einsum("bsh,ch->bsc", grad_chan_pre, w_chan1,
                                     preferred_element_type=jnp.float32).astype(jnp.bfloat16)
        (grad_mid_ln,) = ln2_pull(grad_normed_mid)
        grad_mid = grad_loc + grad_mid_ln
        grad_mid_cols = lax.all_to_all(grad_mid, "seq", 2, 1, tiled=True)
        grad_wtok2 = jnp.einsum("bdc,bsc->ds", tok_act, grad_mid_cols, preferred_element_type=jnp.float32)
        grad_tok_act = jnp.einsum("bsc,ds->bdc", grad_mid_cols, w_tok2,
                                  preferred_element_type=jnp.float32).astype(jnp.bfloat16)
        (grad_tok_pre,) = tok_pull(grad_tok_act)
        grad_wtok1 = jnp.einsum("bsc,bdc->sd", normed_cols, grad_tok_pre, preferred_element_type=jnp.float32)
        grad_normed_cols = jnp.einsum("bdc,sd->bsc", grad_tok_pre, w_tok1,
                                      preferred_element_type=jnp.float32).astype(jnp.bfloat16)
        grad_normed = lax.all_to_all(grad_normed_cols, "seq", 1, 2, tiled=True)
        (grad_in_ln,) = ln1_pull(grad_normed)
        grad_in = grad_mid + grad_in_ln
        weight_grads = lax.psum((grad_wtok1, grad_wtok2, grad_wchan1, grad_wchan2), "seq")
        return (act_out, grad_in) + tuple(weight_grads)

    return jax.shard_map(device_step, mesh=mesh, in_specs=spec_in, out_specs=spec_out, check_vma=False)
```

profile of v0, /device:TPU:0, one launch (start us, length us, event | category | flops | bytes accessed | tf_op | source)
XLA Modules:
  0.0 2087.2 jit_solution(6025338705968842815)
XLA Ops:
  37.8 33.9 %copy.34 = bf16[64,144,768]{1,0,2:T(8,128)(2,1)} copy(bf16[64,144,768]{2,1,0:T(8,128)(2,1)} %fusion.22) | data formatting | bytes 28311552 | tf_op jit(solution)/shard_map/jvp()/convert_element_type | solution.py:14
  71.6 288.6 %all_to_all.54 = bf16[64,144,768]{1,0,2:T(8,128)(2,1)} all-to-all(bf16[64,144,768]{1,0,2:T(8,128)(2,1)} %copy.34), channel_id=1, replica_groups=mesh['data'=2,'seq'=4] {'seq'}, dimensions={2} | all-to-all | bytes 28311552 | tf_op jit(solution)/shard_map/all_to_all | solution.py:30
  360.3 33.2 %copy.35 = bf16[64,144,4,192]{3,1,2,0:T(8,128)(2,1)} copy(bf16[64,144,4,192]{1,0,3,2:T(8,128)(2,1)} %bitcast.96) | data formatting | bytes 28311552 | tf_op jit(solution)/shard_map/all_to_all | solution.py:30
  393.5 16.1 add_convert_fusion.4
  409.6 16.9 fusion.43
  426.5 29.1 %copy.37 = bf16[64,576,192]{2,0,1:T(8,128)(2,1)} copy(bf16[64,576,192]{1,2,0:T(8,128)(2,1)} %fusion.43) | data formatting | bytes 28311552 | tf_op jit(solution)/shard_map/convert_element_type | solution.py:35
  455.6 219.4 %all_to_all.55 = bf16[64,576,192]{2,0,1:T(8,128)(2,1)S(1)} all-to-all(bf16[64,576,192]{2,0,1:T(8,128)(2,1)} %copy.37), channel_id=1, replica_groups=mesh['data'=2,'seq'=4] {'seq'}, dimensions={1} | all-to-all | bytes 28311552 | tf_op jit(solution)/shard_map/all_to_all | solution.py:36
  675.0 34.4 %copy.38 = bf16[64,576,192]{2,1,0:T(8,128)(2,1)S(1)} copy(bf16[64,576,192]{2,0,1:T(8,128)(2,1)S(1)} %all_to_all.55) | data formatting | bytes 28311552 | tf_op jit(solution)/shard_map/all_to_all | solution.py:36
  722.8 42.9 %copy.39 = f32[64,144,4,192]{3,2,1,0:T(4,128)} copy(f32[64,144,4,192]{3,1,2,0:T(8,128)} %convert_bitcast_fusion.1) | data formatting | bytes 56623104 | tf_op jit(solution)/shard_map/convert_element_type | solution.py:37
  765.7 39.6 %reshape.76 = f32[64,144,768]{2,1,0:T(8,128)} reshape(f32[64,144,4,192]{3,2,1,0:T(4,128)} %copy.39) | data formatting | bytes 56623104 | tf_op jit(solution)/shard_map/convert_element_type | solution.py:37
  831.1 54.4 %add_convert_fusion = bf16[64,144,3072]{2,1,0:T(8,128)(2,1)} fusion(f32[3072]{0:T(1024)S(1)} %copy-done.27, bf16[64,144,768]{2,1,0:T(8,128)(2,1)} %copy-done.2, f32[768]{0:T(1024)S(1)} %copy-done.30, f32[768]{0:T(1024)S(1)} %copy-done.21, f32[64,144]{1,0:T(8,128)S(1)} %fusion.62, f32[64,144]{1,0:T(8,128)S(1)} %broadcast_multiply_fusion, ...), kind=kOutput, calls=%fused_computation.17 | convolution fusion | flops 43585634304 | bytes 75589632 | tf_op jit(solution)/shard_map/bsc,ch->bsh/dot_general | solution.py:39
  885.5 109.9 %fusion.3 = bf16[64,144,3072]{2,1,0:T(8,128)(2,1)} fusion(bf16[64,144,3072]{2,1,0:T(8,128)(2,1)} %add_convert_fusion, bf16[64,144,768]{2,1,0:T(8,128)(2,1)} %param.15, bf16[3072,768]{1,0:T(8,128)(2,1)} %param.26), kind=kOutput, calls=%fused_computation.9 | convolution fusion | flops 44137709568 | bytes 132120576 | tf_op jit(solution)/shard_map/bsc,hc->bsh/dot_general | solution.py:46
  995.5 60.9 %fusion.29 = (f32[64,144]{1,0:T(8,128)S(1)}, bf16[64,144,768]{2,1,0:T(8,128)(2,1)}) fusion(bf16[64,144,768]{2,1,0:T(8,128)(2,1)} %copy-done.2, f32[768]{0:T(1024)S(1)} %copy-done.22, f32[64,144]{1,0:T(8,128)} %copy-done.9, bf16[64,144,3072]{2,1,0:T(8,128)(2,1)} %fusion.3, bf16[768,3072]{1,0:T(8,128)(2,1)} %param.24), kind=kOutput, calls=%fused_computation.47 | convolution fusion | flops 43536080896 | bytes 89730048 | tf_op jit(solution)/shard_map/bsh,ch->bsc/dot_general | solution.py:50
  1056.5 18.3 fusion.42
  1074.9 14.7 fusion.44
  1089.6 34.1 %copy.40 = bf16[64,144,768]{1,0,2:T(8,128)(2,1)} copy(bf16[64,144,768]{2,1,0:T(8,128)(2,1)} %fusion.44) | data formatting | bytes 28311552 | tf_op jit(solution)/shard_map/add | solution.py:53
  1132.2 76.7 %fusion.30 = bf16[64,144,768]{2,1,0:T(8,128)(2,1)} fusion(bf16[64,144,768]{2,1,0:T(8,128)(2,1)} %copy-done.2, f32[768]{0:T(1024)S(1)} %copy-done.29, bf16[3072,768]{1,0:T(8,128)(2,1)} %param.26, bf16[64,144,3072]{2,1,0:T(8,128)(2,1)} %add_convert_fusion), kind=kOutput, calls=%fused_computation.48 | convolution fusion | flops 43797970944 | bytes 89656320 | tf_op jit(solution)/shard_map/bsh,hc->bsc/dot_general | solution.py:42
  1208.9 195.9 %all-to-all-done.2 = bf16[64,144,768]{1,0,2:T(8,128)(2,1)} async-done(((bf16[64,144,768]{1,0,2:T(8,128)(2,1)}), bf16[64,144,768]{1,0,2:T(8,128)(2,1)}, u32[]{:S(2)}, u32[]{:S(2)}) %all-to-all-start.2) | async-done | bytes 14155808 | tf_op jit(solution)/shard_map/all_to_all | solution.py:54
  1404.8 33.2 %copy.41 = bf16[64,144,4,192]{3,1,2,0:T(8,128)(2,1)} copy(bf16[64,144,4,192]{1,0,3,2:T(8,128)(2,1)} %bitcast.11) | data formatting | bytes 28311552 | tf_op jit(solution)/shard_map/all_to_all | solution.py:54
  1437.9 28.3 %fusion.37 = bf16[64,384,192]{1,2,0:T(8,128)(2,1)} fusion(bf16[64,192,384]{2,1,0:T(8,128)(2,1)} %add_convert_fusion.4, bf16[64,576,192]{2,1,0:T(8,128)(2,1)} %bitcast.101, bf16[384,576]{0,1:T(8,128)(2,1)S(1)} %copy-done), kind=kOutput, calls=%fused_computation.60 | convolution fusion | flops 5544345600 | bytes 33472512 | tf_op jit(solution)/shard_map/bsc,ds->bdc/dot_general | solution.py:56
  1466.3 15.2 convert_bitcast_fusion.2
  1481.5 28.2 %copy.43 = bf16[64,576,192]{2,0,1:T(8,128)(2,1)} copy(bf16[64,576,192]{1,2,0:T(8,128)(2,1)} %convert_bitcast_fusion.2) | data formatting | bytes 28311552 | tf_op jit(solution)/shard_map/convert_element_type | solution.py:61
  1517.1 63.1 %convolution_bitcast_fusion = f32[3072,768]{1,0:T(8,128)} fusion(bf16[64,144,768]{2,1,0:T(8,128)(2,1)} %param.15, bf16[64,144,3072]{2,1,0:T(8,128)(2,1)} %add_convert_fusion), kind=kOutput, calls=%fused_computation.78 | convolution fusion | flops 43769659392 | bytes 80216064 | tf_op jit(solution)/shard_map/bsh,bsc->hc/dot_general | solution.py:45
  1580.3 56.6 %fusion.50 = f32[768,3072]{1,0:T(8,128)} fusion(bf16[64,144,3072]{2,1,0:T(8,128)(2,1)} %fusion.3, bf16[64,144,768]{2,1,0:T(8,128)(2,1)} %copy-done.2, f32[768]{0:T(1024)S(1)} %copy-done.31, f32[768]{0:T(1024)S(1)} %copy-done.23, f32[64,144]{1,0:T(8,128)S(1)} %copy-done.14, f32[64,144]{1,0:T(8,128)S(1)} %copy-done.11), kind=kOutput, calls=%fused_computation.77 | convolution fusion | flops 43529011200 | bytes 80295936 | tf_op jit(solution)/shard_map/bsc,bsh->ch/dot_general | solution.py:49
  1648.1 18.5 convolution_bitcast_fusion.1
  1666.6 104.6 %all-to-all-done.3 = bf16[64,576,192]{2,0,1:T(8,128)(2,1)} async-done(((bf16[64,576,192]{2,0,1:T(8,128)(2,1)}), bf16[64,576,192]{2,0,1:T(8,128)(2,1)}, u32[]{:S(2)}, u32[]{:S(2)}) %all-to-all-start.3) | async-done | bytes 14155808 | tf_op jit(solution)/shard_map/all_to_all | solution.py:62
  1771.2 17.6 copy.44
  1802.2 43.1 %copy.45 = f32[64,144,4,192]{3,2,1,0:T(4,128)} copy(f32[64,144,4,192]{3,1,2,0:T(8,128)} %convert_bitcast_fusion) | data formatting | bytes 56623104 | tf_op jit(solution)/shard_map/transpose(jvp())/convert_element_type | solution.py:14
  1845.3 39.7 %reshape.77 = f32[64,144,768]{2,1,0:T(8,128)} reshape(f32[64,144,4,192]{3,2,1,0:T(4,128)} %copy.45) | data formatting | bytes 56623104 | tf_op jit(solution)/shard_map/transpose(jvp())/convert_element_type | solution.py:14
  1885.0 19.1 fusion.23
  1918.6 25.2 %fusion.45 = bf16[64,144,768]{2,1,0:T(8,128)(2,1)} fusion(bf16[64,144,768]{2,1,0:T(8,128)(2,1)} %fusion.44, f32[64,144]{1,0:T(8,128)S(1)} %negate_multiply_fusion, f32[64,144]{1,0:T(8,128)S(1)} %multiply_multiply_fusion.2, f32[64,144]{1,0:T(8,128)S(1)} %copy-done.6, bf16[64,144,768]{2,1,0:T(8,128)(2,1)} %param.14, f32[64,144]{1,0:T(8,128)S(1)} %copy-done.8, ...), kind=kLoop, calls=%fused_computation.73 | loop fusion | flops 70778880 | bytes 70929408 | tf_op jit(solution)/shard_map/add | solution.py:64
  1943.8 119.3 %all-reduce.3.cloned.1.call-done = (f32[576,384]{1,0:T(8,128)}, f32[384,576]{0,1:T(8,128)}, f32[768,3072]{1,0:T(8,128)}, f32[3072,768]{1,0:T(8,128)}) async-done(((f32[576,384]{1,0:T(8,128)}, f32[384,576]{0,1:T(8,128)}, f32[768,3072]{1,0:T(8,128)}, f32[3072,768]{1,0:T(8,128)}), (f32[576,384]{1,0:T(8,128)}, f32[384,576]{0,1:T(8,128)}, f32[768,3072]{1,0:T(8,128)}, ...) | async-done | bytes 20643856 | tf_op jit(solution)/shard_map/psum | solution.py:65
  (107 shorter events, 141.7 us)
Async XLA Ops:
  7.2 402.4 %copy-start = (bf16[384,576]{0,1:T(8,128)(2,1)S(1)}, bf16[384,576]{0,1:T(8,128)(2,1)}, u32[]{:S(2)}) copy-start(bf16[384,576]{0,1:T(8,128)(2,1)} %param.20) | copy-start | bytes 1327108
  360.2 33.2 %copy-start.25 = (bf16[576,384]{1,0:T(8,128)(2,1)S(1)}, bf16[576,384]{1,0:T(8,128)(2,1)}, u32[]{:S(2)}) copy-start(bf16[576,384]{1,0:T(8,128)(2,1)} %param.18) | copy-start | bytes 1327108
  360.2 33.2 %copy-start.32 = (f32[384]{0:T(512)S(1)}, f32[384]{0:T(512)}, u32[]{:S(2)}) copy-start(f32[384]{0:T(512)} %param.19) | copy-start | bytes 4612
  393.5 16.1 copy-start.28
  805.3 25.7 %copy-start.21 = (f32[768]{0:T(1024)S(1)}, f32[768]{0:T(1024)}, u32[]{:S(2)}) copy-start(f32[768]{0:T(1024)} %param.22) | copy-start | bytes 9220
  805.3 25.8 %copy-start.27 = (f32[3072]{0:T(1024)S(1)}, f32[3072]{0:T(1024)}, u32[]{:S(2)}) copy-start(f32[3072]{0:T(1024)} %param.25) | copy-start | bytes 36868
  805.3 25.8 %copy-start.30 = (f32[768]{0:T(1024)S(1)}, f32[768]{0:T(1024)}, u32[]{:S(2)}) copy-start(f32[768]{0:T(1024)} %param.23) | copy-start | bytes 9220
  819.7 65.8 %copy-start.9 = (f32[64,144]{1,0:T(8,128)}, f32[64,144]{1,0:T(8,128)S(1)}, u32[]{:S(2)}) copy-start(f32[64,144]{1,0:T(8,128)S(1)} %broadcast_multiply_fusion) | copy-start | bytes 110596
  831.1 54.4 %copy-start.12 = (f32[64,144]{1,0:T(8,128)}, f32[64,144]{1,0:T(8,128)S(1)}, u32[]{:S(2)}) copy-start(f32[64,144]{1,0:T(8,128)S(1)} %fusion.62) | copy-start | bytes 110596
  885.5 109.9 %copy-start.22 = (f32[768]{0:T(1024)S(1)}, f32[768]{0:T(1024)}, u32[]{:S(2)}) copy-start(f32[768]{0:T(1024)} %param.22) | copy-start | bytes 9220
  995.4 60.9 %copy-start.18 = (f32[64,144]{1,0:T(8,128)S(1)}, f32[64,144]{1,0:T(8,128)}, u32[]{:S(2)}) copy-start(f32[64,144]{1,0:T(8,128)} %copy-done.17) | copy-start | bytes 110596
  995.4 61.0 %copy-start.10 = (f32[64,144]{1,0:T(8,128)S(1)}, f32[64,144]{1,0:T(8,128)}, u32[]{:S(2)}) copy-start(f32[64,144]{1,0:T(8,128)} %copy-done.9) | copy-start | bytes 110596
  995.4 61.0 %copy-start.13 = (f32[64,144]{1,0:T(8,128)S(1)}, f32[64,144]{1,0:T(8,128)}, u32[]{:S(2)}) copy-start(f32[64,144]{1,0:T(8,128)} %copy-done.12) | copy-start | bytes 110596
  1056.4 18.5 slice-start
  1056.4 18.5 copy-start.3
  1056.4 18.4 slice-start.1
  1056.4 18.4 slice-start.2
  1056.4 18.4 slice-start.3
  1123.7 281.1 %all-to-all-start.2 = ((bf16[64,144,768]{1,0,2:T(8,128)(2,1)}), bf16[64,144,768]{1,0,2:T(8,128)(2,1)}, u32[]{:S(2)}, u32[]{:S(2)}) async-start(bf16[64,144,768]{1,0,2:T(8,128)(2,1)} %copy.40), calls=%async_computation.2 | async-start | bytes 50331648 | tf_op jit(solution)/shard_map/all_to_all | solution.py:54
  1437.9 28.4 %copy-start.26 = (bf16[576,384]{1,0:T(8,128)(2,1)S(1)}, bf16[576,384]{1,0:T(8,128)(2,1)}, u32[]{:S(2)}) copy-start(bf16[576,384]{1,0:T(8,128)(2,1)} %param.18) | copy-start | bytes 1327108
  1509.7 261.5 %all-to-all-start.3 = ((bf16[64,576,192]{2,0,1:T(8,128)(2,1)}), bf16[64,576,192]{2,0,1:T(8,128)(2,1)}, u32[]{:S(2)}, u32[]{:S(2)}) async-start(bf16[64,576,192]{2,0,1:T(8,128)(2,1)} %copy.43), calls=%async_computation.3 | async-start | bytes 37748736 | tf_op jit(solution)/shard_map/all_to_all | solution.py:62
  1517.0 63.2 %copy-start.11 = (f32[64,144]{1,0:T(8,128)S(1)}, f32[64,144]{1,0:T(8,128)}, u32[]{:S(2)}) copy-start(f32[64,144]{1,0:T(8,128)} %copy-done.9) | copy-start | bytes 110596
  1517.0 63.2 %copy-start.14 = (f32[64,144]{1,0:T(8,128)S(1)}, f32[64,144]{1,0:T(8,128)}, u32[]{:S(2)}) copy-start(f32[64,144]{1,0:T(8,128)} %copy-done.12) | copy-start | bytes 110596
  1517.0 63.2 %copy-start.23 = (f32[768]{0:T(1024)S(1)}, f32[768]{0:T(1024)}, u32[]{:S(2)}) copy-start(f32[768]{0:T(1024)} %param.22) | copy-start | bytes 9220
  1517.0 63.2 %copy-start.31 = (f32[768]{0:T(1024)S(1)}, f32[768]{0:T(1024)}, u32[]{:S(2)}) copy-start(f32[768]{0:T(1024)} %param.23) | copy-start | bytes 9220
  1517.1 546.1 %all-reduce.3.cloned.1.call-start = ((), (), s32[]{:S(2)}) async-start(), calls=%async_computation.4 | async-start | bytes 41287680 | tf_op jit(solution)/shard_map/psum | solution.py:65
  1580.2 56.6 %copy-start.4 = (bf16[64,144,4,192]{3,1,2,0:T(8,128)(2,1)S(1)}, bf16[64,144,4,192]{3,1,2,0:T(8,128)(2,1)}, u32[]{:S(2)}) copy-start(bf16[64,144,4,192]{3,1,2,0:T(8,128)(2,1)} %copy.35) | copy-start | bytes 42467332
  1845.3 39.7 %copy-start.6 = (f32[64,144]{1,0:T(8,128)S(1)}, f32[64,144]{1,0:T(8,128)}, u32[]{:S(2)}) copy-start(f32[64,144]{1,0:T(8,128)} %copy-done.5) | copy-start | bytes 110596
  1845.3 39.7 %copy-start.20 = (f32[768]{0:T(1024)S(1)}, f32[768]{0:T(1024)}, u32[]{:S(2)}) copy-start(f32[768]{0:T(1024)} %param.16) | copy-start | bytes 9220
  1885.0 19.1 copy-start.16
  1885.0 21.3 %copy-start.1 = (f32[64,144,768]{2,1,0:T(8,128)S(1)}, f32[64,144,768]{2,1,0:T(8,128)}, u32[]{:S(2)}) copy-start(f32[64,144,768]{2,1,0:T(8,128)} %reshape.77) | copy-start | bytes 84934656
  1885.0 21.3 %copy-start.8 = (f32[64,144]{1,0:T(8,128)S(1)}, f32[64,144]{1,0:T(8,128)}, u32[]{:S(2)}) copy-start(f32[64,144]{1,0:T(8,128)} %copy-done.7) | copy-start | bytes 110596
  (11 other events, 86.6 us)
Sparse Core Ops, SparseCore 0:
  1666.7 396.4 all-reduce.2
where the time goes:
time: 2090 us
  matrix products  528 us (25%)
  blocking collectives  508 us (24%)
  local copies, waits for them, and re-layouts  435 us (21%)
  waiting for transfers between devices  420 us (20%)
  other arithmetic  166 us (8%)
    all_to_all x1, blocking collectives, device_step(): normed_cols = lax.all_to_all(normed, 'seq', 2, 1, tiled=True)  289 us
    all_to_all x1, blocking collectives, device_step(): tok_rows = lax.all_to_all(tok_cols, 'seq', 1, 2, tiled=True)  219 us
    all_to_all x1, waiting for transfers between devices, device_step(): grad_mid_cols = lax.all_to_all(grad_mid, 'seq', 2, 1, tiled=True)  196 us
    psum x1, waiting for transfers between devices, device_step(): lax.psum((grad_wtok1, grad_wtok2, grad_wchan1, grad_wchan2), 'seq')  119 us
    convert_element_type x3, local copies, waits for them, and re-layouts, layer_norm(): (centered * lax.rsqrt(row_var + LN_EPS) * ln_scale + ln_shift).astype(jnp...  117 us
    dot_general x1, matrix products, device_step(): jnp.einsum('bsc,hc->bsh', grad_loc, w_chan2, preferred_element_type=jnp.f...  110 us
    all_to_all x1, waiting for transfers between devices, device_step(): grad_normed = lax.all_to_all(grad_normed_cols, 'seq', 1, 2, tiled=True)  105 us
    convert_element_type x2, local copies, waits for them, and re-layouts, device_step(): tok_rows.astype(jnp.float32)  82.5 us
  transfers between devices with their start and end apart: 3, of which 3 were waited for; matrix products, arithmetic and copies ran while one was open for 19% of the time, Pallas kernels for 0%

commit v1 on v0

v1 whole, which is shorter than its diff:
```python
import functools

import jax
import jax.numpy as jnp
from jax import lax
from jax.experimental import pallas as pl
from jax.experimental.pallas import tpu as pltpu
from jax.sharding import PartitionSpec as P


LN_EPS = 1e-6
GELU_C = 0.7978845608028654
GELU_K = 0.044715
F32 = jnp.float32
BF16 = jnp.bfloat16

CHUNK_SIZES = (2, 4, 4, 4, 2)
PIECES = 3
HID_BLOCK = 512
ROW_BLOCK = 48
COL_BLOCK = 256


def gelu_parts(pre):
    sq = pre * pre
    th = jnp.tanh(pre * (GELU_C + (GELU_C * GELU_K) * sq))
    half = 0.5 * pre
    cdf = 0.5 + 0.5 * th
    slope = cdf + (half * (1.0 - th * th)) * (GELU_C + (3.0 * GELU_C * GELU_K) * sq)
    return pre * cdf, slope


def gelu_value(pre):
    sq = pre * pre
    th = jnp.tanh(pre * (GELU_C + (GELU_C * GELU_K) * sq))
    return pre * (0.5 + 0.5 * th)


def gelu_slope(pre):
    return gelu_parts(pre)[1]


def dot(a, b):
    return jnp.dot(a, b, preferred_element_type=F32)


def dot_nt(a, b):
    return lax.dot_general(a, b, (((1,), (1,)), ((), ())), preferred_element_type=F32)


def layer_kernel(first, *refs):
    x_refs, dz_refs = refs[0:4], refs[4:8]
    (ln1_s, ln1_b, ln2_s, ln2_b, b_c1, b_c2, b_t1, b_t2, w_t1, w_t1t, w_t2, w_t2t,
     w_c1, w_c2) = refs[8:22]
    pos = 22
    if not first:
        acc_in = refs[pos:pos + 4]
        pos += 4
    z_refs, dx_refs = refs[pos:pos + 4], refs[pos + 4:pos + 8]
    acc_out = refs[pos + 8:pos + 12]
    (g_c1, g_c2, g_t1, g_t2, u_s, v_s, vt_s, dz_s, h_s, g_s, x1_s, dv_s, acc_s, sem) = refs[pos + 12:]
    accs = (g_t1, g_t2, g_c1, g_c2)
    step = pl.program_id(0)
    rows = x_refs[0].shape[1]
    total_rows = 4 * rows
    chans = u_s.shape[1]
    hid = w_c1.shape[1]

    @pl.when(step == 0)
    def _():
        if first:
            for acc in accs:
                acc[...] = jnp.zeros_like(acc)
        else:
            copies = [pltpu.make_async_copy(src, acc, sem.at[i])
                      for i, (src, acc) in enumerate(zip(acc_in, accs))]
            for cp in copies:
                cp.start()
            for cp in copies:
                cp.wait()

    def norm(val, scale, shift):
        mean = jnp.mean(val, axis=-1, keepdims=True)
        cen = val - mean
        var = jnp.mean(cen * cen, axis=-1, keepdims=True)
        return (cen * lax.rsqrt(var + LN_EPS) * scale + shift).astype(BF16)

    def norm_grad(val, grad, scale):
        mean = jnp.mean(val, axis=-1, keepdims=True)
        cen = val - mean
        var = jnp.mean(cen * cen, axis=-1, keepdims=True)
        inv = lax.rsqrt(var + LN_EPS)
        hat = cen * inv
        gs = grad * scale
        m1 = jnp.mean(gs, axis=-1, keepdims=True)
        m2 = jnp.mean(gs * hat, axis=-1, keepdims=True)
        return (inv * (gs - m1 - hat * m2)).astype(BF16)

    per_block = rows // ROW_BLOCK

    for k in range(4):
        def ln1_step(i, carry, k=k):
            r = pl.multiple_of(i * ROW_BLOCK, 16)
            dst = pl.ds(k * rows + r, ROW_BLOCK)
            u_s[dst, :] = norm(x_refs[k][0, pl.ds(r, ROW_BLOCK), :].astype(F32), ln1_s[...], ln1_b[...])
            dz_s[dst, :] = dz_refs[k][0, pl.ds(r, ROW_BLOCK), :]
            return carry

        lax.fori_loop(0, per_block, ln1_step, 0, unroll=True)

    for n in range(chans // COL_BLOCK):
        cols = slice(n * COL_BLOCK, (n + 1) * COL_BLOCK)
        h = (dot(w_t1t[...], u_s[:, cols]) + b_t1[...]).astype(BF16)
        h_s[:, cols] = h
        g = gelu_value(h.astype(F32)).astype(BF16)
        g_s[:, cols] = g
        t = (dot(w_t2t[...], g) + b_t2[...]).astype(BF16)
        for k in range(4):
            part = slice(k * rows, (k + 1) * rows)
            x1_s[part, cols] = (x_refs[k][0, :, cols].astype(F32) + t[part].astype(F32)).astype(BF16)

    def ln2_step(i, carry):
        r = pl.ds(pl.multiple_of(i * ROW_BLOCK, 16), ROW_BLOCK)
        v_s[r, :] = norm(x1_s[r, :].astype(F32), ln2_s[...], ln2_b[...])
        return carry

    lax.fori_loop(0, total_rows // ROW_BLOCK, ln2_step, 0, unroll=True)

    vt_s[...] = v_s[...].T
    acc_s[...] = jnp.zeros_like(acc_s)
    dv_s[...] = jnp.zeros_like(dv_s)

    def hid_step(j, carry):
        cols = pl.ds(pl.multiple_of(j * HID_BLOCK, HID_BLOCK), HID_BLOCK)
        v = v_s[...]
        dz = dz_s[...]
        a = (dot(v, w_c1[:, cols]) + b_c1[:, cols]).astype(BF16)
        q32, slope = gelu_parts(a.astype(F32))
        q = q32.astype(BF16)
        dq = dot_nt(dz, w_c2[cols, :]).astype(BF16)
        da = (dq.astype(F32) * slope).astype(BF16)
        acc_s[...] += dot(q, w_c2[cols, :])
        dv_s[...] += dot_nt(da, w_c1[:, cols])
        g_c1[:, cols] += dot(vt_s[...], da)
        g_c2[cols, :] += dot(q.T, dz)
        return carry

    lax.fori_loop(0, hid // HID_BLOCK, hid_step, 0)

    for k in range(4):
        def ln2_back(i, carry, k=k):
            r = pl.multiple_of(i * ROW_BLOCK, 16)
            src = pl.ds(k * rows + r, ROW_BLOCK)
            x1 = x1_s[src, :].astype(F32)
            z_refs[k][0, pl.ds(r, ROW_BLOCK), :] = (x1 + (acc_s[src, :] + b_c2[...])).astype(BF16)
            dln = norm_grad(x1, dv_s[src, :].astype(BF16).astype(F32), ln2_s[...])
            v_s[src, :] = (dz_s[src, :].astype(F32) + dln.astype(F32)).astype(BF16)
            return carry

        lax.fori_loop(0, per_block, ln2_back, 0, unroll=True)

    g_t2[...] += dot_nt(g_s[...], v_s[...])
    for n in range(chans // COL_BLOCK):
        cols = slice(n * COL_BLOCK, (n + 1) * COL_BLOCK)
        dg = dot(w_t2[...], v_s[:, cols]).astype(BF16)
        dh = (dg.astype(F32) * gelu_slope(h_s[:, cols].astype(F32))).astype(BF16)
        g_s[:, cols] = dh
        dv_s[:, cols] = dot(w_t1[...], dh)
    g_t1[...] += dot_nt(u_s[...], g_s[...])

    for k in range(4):
        def ln1_back(i, carry, k=k):
            r = pl.multiple_of(i * ROW_BLOCK, 16)
            src = pl.ds(k * rows + r, ROW_BLOCK)
            x = x_refs[k][0, pl.ds(r, ROW_BLOCK), :].astype(F32)
            dln = norm_grad(x, dv_s[src, :].astype(BF16).astype(F32), ln1_s[...])
            dx_refs[k][0, pl.ds(r, ROW_BLOCK), :] = (v_s[src, :].astype(F32) + dln.astype(F32)).astype(BF16)
            return carry

        lax.fori_loop(0, per_block, ln1_back, 0, unroll=True)

    @pl.when(step == pl.num_programs(0) - 1)
    def _():
        copies = [pltpu.make_async_copy(acc, dst, sem.at[i])
                  for i, (acc, dst) in enumerate(zip(accs, acc_out))]
        for cp in copies:
            cp.start()
        for cp in copies:
            cp.wait()


def layer_call(xs, dzs, params, accs):
    images, rows, chans = xs[0].shape
    w_t1, w_c1 = params[8], params[12]
    total_rows, tok_hid = w_t1.shape
    hid = w_c1.shape[1]
    first = accs is None
    block = pl.BlockSpec((1, rows, chans), lambda i: (i, 0, 0))
    whole = pl.BlockSpec(memory_space=pltpu.VMEM)
    anywhere = pl.BlockSpec(memory_space=pl.ANY)
    acc_shapes = [(total_rows, tok_hid), (tok_hid, total_rows), (chans, hid), (hid, chans)]
    act = jax.ShapeDtypeStruct((images, rows, chans), BF16)
    out_shape = [act] * 8 + [jax.ShapeDtypeStruct(s, F32) for s in acc_shapes]
    n_in = 8 + len(params)
    acc_args = () if first else tuple(accs)
    flops = images * (12 * total_rows * chans * hid + 12 * total_rows * chans * tok_hid)
    return pl.pallas_call(
        functools.partial(layer_kernel, first),
        grid=(images,),
        in_specs=[block] * 8 + [whole] * len(params) + [anywhere] * len(acc_args),
        out_specs=[block] * 8 + [anywhere] * 4,
        out_shape=out_shape,
        scratch_shapes=[
            pltpu.VMEM(acc_shapes[2], F32), pltpu.VMEM(acc_shapes[3], F32),
            pltpu.VMEM(acc_shapes[0], F32), pltpu.VMEM(acc_shapes[1], F32),
            pltpu.VMEM((total_rows, chans), BF16), pltpu.VMEM((total_rows, chans), BF16),
            pltpu.VMEM((chans, total_rows), BF16), pltpu.VMEM((total_rows, chans), BF16),
            pltpu.VMEM((tok_hid, chans), BF16), pltpu.VMEM((tok_hid, chans), BF16),
            pltpu.VMEM((total_rows, chans), BF16),
            pltpu.VMEM((total_rows, chans), F32), pltpu.VMEM((total_rows, chans), F32),
            pltpu.SemaphoreType.DMA((4,)),
        ],
        input_output_aliases={} if first else {n_in + i: 8 + i for i in range(4)},
        compiler_params=pltpu.CompilerParams(
            dimension_semantics=("arbitrary",), vmem_limit_bytes=66_000_000),
        cost_estimate=pl.CostEstimate(flops=flops, bytes_accessed=60_000_000, transcendentals=0),
    )(*xs, *dzs, *params, *acc_args)


def solution(mesh):
    act_spec = P("data", "seq", None)
    part_spec = P("data", None)
    spec_in = (act_spec, act_spec) + (P(),) * 12
    spec_out = (act_spec, act_spec, part_spec, part_spec, part_spec, part_spec)
    ranks = mesh.shape["seq"]

    def hop(val, dist):
        return lax.ppermute(val, "seq", [(i, i ^ dist) for i in range(ranks)])

    def device_body(act_loc, grad_loc, ln1_scale, ln1_shift, w_tok1, b_tok1, w_tok2, b_tok2,
                    ln2_scale, ln2_shift, w_chan1, b_chan1, w_chan2, b_chan2):
        me = lax.axis_index("seq")
        core = me % 2
        images, rows, _ = act_loc.shape
        own = images // ranks

        def permute_blocks(arr, axis):
            parts = [lax.dynamic_slice_in_dim(arr, (me ^ d) * rows, rows, axis) for d in range(ranks)]
            return jnp.concatenate(parts, axis)

        w_t1 = permute_blocks(w_tok1, 0)
        w_t2 = permute_blocks(w_tok2, 1)
        b_t2 = permute_blocks(b_tok2, 0)
        params = (ln1_scale[None], ln1_shift[None], ln2_scale[None], ln2_shift[None], b_chan1[None], b_chan2[None],
                  b_tok1[:, None], b_t2[:, None], w_t1, w_t1.T, w_t2, w_t2.T,
                  w_chan1, w_chan2)

        def fetch(arr, start, size):
            blocks = []
            for d in range(ranks):
                piece = lax.dynamic_slice_in_dim(arr, (me ^ d) * own + start, size, 0)
                blocks.append(piece if d == 0 else hop(piece, d))
            return blocks

        starts = [sum(CHUNK_SIZES[:c]) for c in range(len(CHUNK_SIZES))]
        ins = [(fetch(act_loc, s, n), fetch(grad_loc, s, n))
               for s, n in zip(starts, CHUNK_SIZES)]
        act_out = jnp.zeros_like(act_loc)
        grad_in = jnp.zeros_like(act_loc)
        accs = None
        for c, offset in enumerate(starts):
            outs = layer_call(ins[c][0], ins[c][1], params, accs)
            accs = outs[8:]
            for d in range(ranks):
                z, dx = outs[d], outs[4 + d]
                if d:
                    z, dx = hop(z, d), hop(dx, d)
                start = (me ^ d) * own + offset
                act_out = lax.dynamic_update_slice_in_dim(act_out, z, start, 0)
                grad_in = lax.dynamic_update_slice_in_dim(grad_in, dx, start, 0)

        def group_sum(part, pieces):
            half = part.shape[0] // 2
            size = half // pieces
            out = jnp.zeros_like(part)
            for p in range(pieces):
                mine_at, other_at = core * half + p * size, (1 - core) * half + p * size
                mine = lax.dynamic_slice_in_dim(part, mine_at, size, 0)
                other = lax.dynamic_slice_in_dim(part, other_at, size, 0)
                pair = mine + hop(other, 1)
                full = pair + hop(pair, 2)
                peer = hop(full, 1)
                out = lax.dynamic_update_slice_in_dim(out, full, mine_at, 0)
                out = lax.dynamic_update_slice_in_dim(out, peer, other_at, 0)
            return out

        g_c1 = group_sum(accs[2], PIECES)
        g_c2 = group_sum(accs[3], PIECES)
        g_t1 = group_sum(permute_blocks(accs[0], 0), 1)
        g_t2 = group_sum(permute_blocks(accs[1], 1), 1)
        return act_out, grad_in, g_t1, g_t2, g_c1, g_c2

    return jax.shard_map(device_body, mesh=mesh, in_specs=spec_in, out_specs=spec_out, check_vma=False)
```

time: 2090 us -> 1220 us (0.58)
  Pallas kernels: 0 us -> 555 us
  matrix products: 528 us -> 0 us
  blocking collectives: 508 us -> 0 us
  local copies, waits for them, and re-layouts: 435 us -> 125 us
  other arithmetic: 166 us -> 25.6 us
  waiting for transfers between devices: 420 us -> 459 us
  starting transfers between devices: 15.9 us -> 53.5 us
    pallas_call x0 -> x5, Pallas kernels: none -> 555 us  [layer_call(): pl.pallas_call(functools.partial(layer_kernel, first), grid=(images,), in...]
    dot_general x12 -> x0, matrix products: 528 us -> none  [the longest x1 110 us: device_step(): jnp.einsum('bsc,hc->bsh', grad_loc, w_chan2, preferred_element_type=jnp.f...]
    all_to_all x2 -> x0, blocking collectives: 508 us -> none  [the longest x1 289 us: device_step(): normed_cols = lax.all_to_all(normed, 'seq', 2, 1, tiled=True)]
    ppermute x0 -> x84, waiting for transfers between devices: none -> 459 us  [hop(): return lax.ppermute(val, 'seq', [(i, i ^ dist) for i in range(ranks)])]
    all_to_all x2 -> x0, waiting for transfers between devices: 300 us -> none  [the longest x1 196 us: device_step(): grad_mid_cols = lax.all_to_all(grad_mid, 'seq', 2, 1, tiled=True)]
    convert_element_type x7 -> x0, local copies, waits for them, and re-layouts: 256 us -> none  [the longest x3 117 us: layer_norm(): (centered * lax.rsqrt(row_var + LN_EPS) * ln_scale + ln_shift).astype(jnp...]
    psum x1 -> x0, waiting for transfers between devices: 119 us -> none  [device_step(): lax.psum((grad_wtok1, grad_wtok2, grad_wchan1, grad_wchan2), 'seq')]
    all_to_all x4 -> x0, local copies, waits for them, and re-layouts: 118 us -> none  [the longest x1 34.4 us: device_step(): tok_rows = lax.all_to_all(tok_cols, 'seq', 1, 2, tiled=True)]
  transfers between devices with their start and end apart: 3 -> 84, of which waited for: 3 -> 24; matrix products, arithmetic and copies ran while one was open for 19% -> 12% of each run, Pallas kernels for 0% -> 39%
where the time goes in v1:
time: 1220 us
  Pallas kernels  555 us (45%)
  waiting for transfers between devices  459 us (38%)
  local copies, waits for them, and re-layouts  125 us (10%)
  starting transfers between devices  53.5 us (4%)
  other arithmetic  25.6 us (2%)
    pallas_call x5, Pallas kernels, layer_call(): pl.pallas_call(functools.partial(layer_kernel, first), grid=(images,), in...  555 us
    ppermute x84, waiting for transfers between devices, hop(): return lax.ppermute(val, 'seq', [(i, i ^ dist) for i in range(ranks)])  459 us
    ppermute x84, starting transfers between devices, hop(): return lax.ppermute(val, 'seq', [(i, i ^ dist) for i in range(ranks)])  53.5 us
  transfers between devices with their start and end apart: 84, of which 24 were waited for; matrix products, arithmetic and copies ran while one was open for 12% of the time, Pallas kernels for 39%

profile of v1, /device:TPU:0, one launch (start us, length us, event | category | flops | bytes accessed | tf_op | source)
XLA Modules:
  0.0 1219.5 jit_solution(4412264808477477978)
XLA Ops:
  13.4 7.8 constant_dynamic-slice_fusion.28
  21.3 7.8 constant_dynamic-slice_fusion.24
  45.4 39.2 %collective-permute-done.5.refs_7_ = bf16[2,144,768]{2,1,0:T(8,128)(2,1)} collective-permute-done((bf16[2,144,768]{2,1,0:T(8,128)(2,1)}, bf16[2,144,768]{2,1,0:T(8,128)(2,1)}, u32[]{:S(2)}, u32[]{:S(2)}) %collective-permute-start.5) | collective-permute-done | bytes 442400 | tf_op jit(solution)/shard_map/ppermute | solution.py:238
  88.3 72.5 %shard_map.181 = (bf16[2,144,768]{2,1,0:T(8,128)(2,1)}, bf16[2,144,768]{2,1,0:T(8,128)(2,1)}, bf16[2,144,768]{2,1,0:T(8,128)(2,1)}, bf16[2,144,768]{2,1,0:T(8,12...) custom-call(bf16[2,144,768]{2,1,0:T(8,128)(2,1)} %get-tuple-element., ...), custom_call_target="tpu_custom_call" | custom-call | flops 36691771392 | bytes 60000000 | tf_op jit(solution)/shard_map/pallas_call | solution.py:207
  163.7 134.6 %shard_map.182 = (bf16[4,144,768]{2,1,0:T(8,128)(2,1)}, bf16[4,144,768]{2,1,0:T(8,128)(2,1)}, bf16[4,144,768]{2,1,0:T(8,128)(2,1)}, bf16[4,144,768]{2,1,0:T(8,12...) custom-call(bf16[4,144,768]{2,1,0:T(8,128)(2,1)} %get-tuple-element., ...), custom_call_target="tpu_custom_call", output_to_operand_aliasing={{8}: (22, {}), {9}: (23, {}), {10}: (24, {}), {11}: (25, {})} | custom-call | flops 73383542784 | bytes 60000000 | tf_op jit(solution)/shard_map/pallas_call | solution.py:207
  301.9 134.6 %shard_map.183 = (bf16[4,144,768]{2,1,0:T(8,128)(2,1)}, bf16[4,144,768]{2,1,0:T(8,128)(2,1)}, bf16[4,144,768]{2,1,0:T(8,128)(2,1)}, bf16[4,144,768]{2,1,0:T(8,12...) custom-call(bf16[4,144,768]{2,1,0:T(8,128)(2,1)} %get-tuple-element., ...), custom_call_target="tpu_custom_call", output_to_operand_aliasing={{8}: (22, {}), {9}: (23, {}), {10}: (24, {}), {11}: (25, {})} | custom-call | flops 73383542784 | bytes 60000000 | tf_op jit(solution)/shard_map/pallas_call | solution.py:207
  440.5 134.8 %shard_map.184 = (bf16[4,144,768]{2,1,0:T(8,128)(2,1)}, bf16[4,144,768]{2,1,0:T(8,128)(2,1)}, bf16[4,144,768]{2,1,0:T(8,128)(2,1)}, bf16[4,144,768]{2,1,0:T(8,12...) custom-call(bf16[4,144,768]{2,1,0:T(8,128)(2,1)} %get-tuple-element., ...), custom_call_target="tpu_custom_call", output_to_operand_aliasing={{8}: (22, {}), {9}: (23, {}), {10}: (24, {}), {11}: (25, {})} | custom-call | flops 73383542784 | bytes 60000000 | tf_op jit(solution)/shard_map/pallas_call | solution.py:207
  576.1 78.1 %shard_map.185 = (bf16[2,144,768]{2,1,0:T(8,128)(2,1)}, bf16[2,144,768]{2,1,0:T(8,128)(2,1)}, bf16[2,144,768]{2,1,0:T(8,128)(2,1)}, bf16[2,144,768]{2,1,0:T(8,12...) custom-call(bf16[2,144,768]{2,1,0:T(8,128)(2,1)} %get-tuple-element., ...), custom_call_target="tpu_custom_call", output_to_operand_aliasing={{8}: (22, {}), {9}: (23, {}), {10}: (24, {}), {11}: (25, {})} | custom-call | flops 36691771392 | bytes 60000000 | tf_op jit(solution)/shard_map/pallas_call | solution.py:207
  659.7 6.2 broadcast.4.clone.1
  667.7 6.2 broadcast.4.clone
  695.6 8.4 collective-permute-done.46
  708.8 7.7 collective-permute-done.47
  724.8 14.4 %collective-permute-done.16 = bf16[4,144,768]{2,1,0:T(8,128)(2,1)S(1)} collective-permute-done((bf16[4,144,768]{2,1,0:T(8,128)(2,1)S(1)}, bf16[4,144,768]{2,1,0:T(8,128)(2,1)S(1)}, u32[]{:S(2)}, u32[]{:S(2)}) %collective-permute-start.16) | collective-permute-done | bytes 884768 | tf_op jit(solution)/shard_map/ppermute | solution.py:238
  739.9 17.0 %collective-permute-done.17 = bf16[4,144,768]{2,1,0:T(8,128)(2,1)S(1)} collective-permute-done((bf16[4,144,768]{2,1,0:T(8,128)(2,1)S(1)}, bf16[4,144,768]{2,1,0:T(8,128)(2,1)S(1)}, u32[]{:S(2)}, u32[]{:S(2)}) %collective-permute-start.17) | collective-permute-done | bytes 884768 | tf_op jit(solution)/shard_map/ppermute | solution.py:238
  762.2 29.6 %collective-permute-done.76 = f32[512,768]{1,0:T(8,128)S(1)} collective-permute-done((f32[512,768]{1,0:T(8,128)S(1)}, f32[512,768]{1,0:T(8,128)S(1)}, u32[]{:S(2)}, u32[]{:S(2)}) %collective-permute-start.76) | collective-permute-done | bytes 1572896 | tf_op jit(solution)/shard_map/ppermute | solution.py:238
  798.3 46.2 %collective-permute-done.25 = bf16[4,144,768]{2,1,0:T(8,128)(2,1)S(1)} collective-permute-done((bf16[4,144,768]{2,1,0:T(8,128)(2,1)S(1)}, bf16[4,144,768]{2,1,0:T(8,128)(2,1)S(1)}, u32[]{:S(2)}, u32[]{:S(2)}) %collective-permute-start.25) | collective-permute-done | bytes 884768 | tf_op jit(solution)/shard_map/ppermute | solution.py:238
  844.5 17.8 %collective-permute-done.26 = bf16[4,144,768]{2,1,0:T(8,128)(2,1)S(1)} collective-permute-done((bf16[4,144,768]{2,1,0:T(8,128)(2,1)S(1)}, bf16[4,144,768]{2,1,0:T(8,128)(2,1)S(1)}, u32[]{:S(2)}, u32[]{:S(2)}) %collective-permute-start.26) | collective-permute-done | bytes 884768 | tf_op jit(solution)/shard_map/ppermute | solution.py:238
  863.8 4.9 broadcast_in_dim.46
  873.0 9.4 collective-permute-done.49
  885.1 15.1 %collective-permute-done.50 = bf16[4,144,768]{2,1,0:T(8,128)(2,1)S(1)} collective-permute-done((bf16[4,144,768]{2,1,0:T(8,128)(2,1)S(1)}, bf16[4,144,768]{2,1,0:T(8,128)(2,1)S(1)}, u32[]{:S(2)}, u32[]{:S(2)}) %collective-permute-start.50) | collective-permute-done | bytes 884768 | tf_op jit(solution)/shard_map/ppermute | solution.py:238
  904.1 31.0 %collective-permute-done.79 = f32[512,768]{1,0:T(8,128)S(1)} collective-permute-done((f32[512,768]{1,0:T(8,128)S(1)}, f32[512,768]{1,0:T(8,128)S(1)}, u32[]{:S(2)}, u32[]{:S(2)}) %collective-permute-start.79) | collective-permute-done | bytes 1572896 | tf_op jit(solution)/shard_map/ppermute | solution.py:238
  941.6 46.1 %collective-permute-done.34 = bf16[4,144,768]{2,1,0:T(8,128)(2,1)S(1)} collective-permute-done((bf16[4,144,768]{2,1,0:T(8,128)(2,1)S(1)}, bf16[4,144,768]{2,1,0:T(8,128)(2,1)S(1)}, u32[]{:S(2)}, u32[]{:S(2)}) %collective-permute-start.34) | collective-permute-done | bytes 884768 | tf_op jit(solution)/shard_map/ppermute | solution.py:238
  991.0 15.7 %collective-permute-done.52 = bf16[4,144,768]{2,1,0:T(8,128)(2,1)S(1)} collective-permute-done((bf16[4,144,768]{2,1,0:T(8,128)(2,1)S(1)}, bf16[4,144,768]{2,1,0:T(8,128)(2,1)S(1)}, u32[]{:S(2)}, u32[]{:S(2)}) %collective-permute-start.52) | collective-permute-done | bytes 884768 | tf_op jit(solution)/shard_map/ppermute | solution.py:238
  1006.7 17.8 %collective-permute-done.53 = bf16[4,144,768]{2,1,0:T(8,128)(2,1)S(1)} collective-permute-done((bf16[4,144,768]{2,1,0:T(8,128)(2,1)S(1)}, bf16[4,144,768]{2,1,0:T(8,128)(2,1)S(1)}, u32[]{:S(2)}, u32[]{:S(2)}) %collective-permute-start.53) | collective-permute-done | bytes 884768 | tf_op jit(solution)/shard_map/ppermute | solution.py:238
  1028.7 14.8 %collective-permute-done.35 = bf16[4,144,768]{2,1,0:T(8,128)(2,1)S(1)} collective-permute-done((bf16[4,144,768]{2,1,0:T(8,128)(2,1)S(1)}, bf16[4,144,768]{2,1,0:T(8,128)(2,1)S(1)}, u32[]{:S(2)}, u32[]{:S(2)}) %collective-permute-start.35) | collective-permute-done | bytes 884768 | tf_op jit(solution)/shard_map/ppermute | solution.py:238
  1052.4 25.9 %collective-permute-done.82 = f32[512,768]{1,0:T(8,128)S(1)} collective-permute-done((f32[512,768]{1,0:T(8,128)S(1)}, f32[512,768]{1,0:T(8,128)S(1)}, u32[]{:S(2)}, u32[]{:S(2)}) %collective-permute-start.82) | collective-permute-done | bytes 1572896 | tf_op jit(solution)/shard_map/ppermute | solution.py:238
  1083.0 48.0 %collective-permute-done.55 = bf16[4,144,768]{2,1,0:T(8,128)(2,1)S(1)} collective-permute-done((bf16[4,144,768]{2,1,0:T(8,128)(2,1)S(1)}, bf16[4,144,768]{2,1,0:T(8,128)(2,1)S(1)}, u32[]{:S(2)}, u32[]{:S(2)}) %collective-permute-start.55) | collective-permute-done | bytes 884768 | tf_op jit(solution)/shard_map/ppermute | solution.py:238
  1134.0 14.8 %collective-permute-done.56 = bf16[4,144,768]{2,1,0:T(8,128)(2,1)S(1)} collective-permute-done((bf16[4,144,768]{2,1,0:T(8,128)(2,1)S(1)}, bf16[4,144,768]{2,1,0:T(8,128)(2,1)S(1)}, u32[]{:S(2)}, u32[]{:S(2)}) %collective-permute-start.56) | collective-permute-done | bytes 884768 | tf_op jit(solution)/shard_map/ppermute | solution.py:238
  1151.7 7.7 collective-permute-done.58
  1160.4 9.5 collective-permute-done.64
  1170.0 9.5 collective-permute-done.61
  1190.6 7.9 collective-permute-done.43
  (327 shorter events, 176.8 us)
Async XLA Ops:
  84.6 76.2 %collective-permute-start.13 = (bf16[4,144,768]{2,1,0:T(8,128)(2,1)}, bf16[4,144,768]{2,1,0:T(8,128)(2,1)}, u32[]{:S(2)}, u32[]{:S(2)}) collective-permute-start(bf16[4,144,768]{2,1,0:T(8,128)(2,1)} %get-tuple-element.165), channel_id=1, source_target_pairs={{0,2},{1,3},{2,0},{3,1},{4,6},{5,7},{6,4},{7,5}} | collective-permute-start | bytes 2654216 | tf_op jit(solution)/shard_map/ppermute | solution.py:238
  86.8 76.2 %collective-permute-start.18 = (bf16[4,144,768]{2,1,0:T(8,128)(2,1)}, bf16[4,144,768]{2,1,0:T(8,128)(2,1)}, u32[]{:S(2)}, u32[]{:S(2)}) collective-permute-start(bf16[4,144,768]{2,1,0:T(8,128)(2,1)} %get-tuple-element.174), channel_id=1, source_target_pairs={{0,1},{1,0},{2,3},{3,2},{4,5},{5,4},{6,7},{7,6}} | collective-permute-start | bytes 2654216 | tf_op jit(solution)/shard_map/ppermute | solution.py:238
  86.8 76.3 %collective-permute-start.19 = (bf16[4,144,768]{2,1,0:T(8,128)(2,1)}, bf16[4,144,768]{2,1,0:T(8,128)(2,1)}, u32[]{:S(2)}, u32[]{:S(2)}) collective-permute-start(bf16[4,144,768]{2,1,0:T(8,128)(2,1)} %get-tuple-element.173), channel_id=1, source_target_pairs={{0,2},{1,3},{2,0},{3,1},{4,6},{5,7},{6,4},{7,5}} | collective-permute-start | bytes 2654216 | tf_op jit(solution)/shard_map/ppermute | solution.py:238
  160.8 137.5 %collective-permute-start.20 = (bf16[4,144,768]{2,1,0:T(8,128)(2,1)}, bf16[4,144,768]{2,1,0:T(8,128)(2,1)}, u32[]{:S(2)}, u32[]{:S(2)}) collective-permute-start(bf16[4,144,768]{2,1,0:T(8,128)(2,1)} %get-tuple-element.172), channel_id=1, source_target_pairs={{0,3},{1,2},{2,1},{3,0},{4,7},{5,6},{6,5},{7,4}} | collective-permute-start | bytes 2654216 | tf_op jit(solution)/shard_map/ppermute | solution.py:238
  161.2 138.6 %collective-permute-start.21 = (bf16[4,144,768]{2,1,0:T(8,128)(2,1)}, bf16[4,144,768]{2,1,0:T(8,128)(2,1)}, u32[]{:S(2)}, u32[]{:S(2)}) collective-permute-start(bf16[4,144,768]{2,1,0:T(8,128)(2,1)} %get-tuple-element.162), channel_id=1, source_target_pairs={{0,1},{1,0},{2,3},{3,2},{4,5},{5,4},{6,7},{7,6}} | collective-permute-start | bytes 2654216 | tf_op jit(solution)/shard_map/ppermute | solution.py:238
  161.5 138.3 %collective-permute-start.22 = (bf16[4,144,768]{2,1,0:T(8,128)(2,1)}, bf16[4,144,768]{2,1,0:T(8,128)(2,1)}, u32[]{:S(2)}, u32[]{:S(2)}) collective-permute-start(bf16[4,144,768]{2,1,0:T(8,128)(2,1)} %get-tuple-element.161), channel_id=1, source_target_pairs={{0,2},{1,3},{2,0},{3,1},{4,6},{5,7},{6,4},{7,5}} | collective-permute-start | bytes 2654216 | tf_op jit(solution)/shard_map/ppermute | solution.py:238
  163.0 137.5 %collective-permute-start.23 = (bf16[4,144,768]{2,1,0:T(8,128)(2,1)}, bf16[4,144,768]{2,1,0:T(8,128)(2,1)}, u32[]{:S(2)}, u32[]{:S(2)}) collective-permute-start(bf16[4,144,768]{2,1,0:T(8,128)(2,1)} %get-tuple-element.160), channel_id=1, source_target_pairs={{0,3},{1,2},{2,1},{3,0},{4,7},{5,6},{6,5},{7,4}} | collective-permute-start | bytes 2654216 | tf_op jit(solution)/shard_map/ppermute | solution.py:238
  163.1 138.9 %collective-permute-start.27 = (bf16[4,144,768]{2,1,0:T(8,128)(2,1)}, bf16[4,144,768]{2,1,0:T(8,128)(2,1)}, u32[]{:S(2)}, u32[]{:S(2)}) collective-permute-start(bf16[4,144,768]{2,1,0:T(8,128)(2,1)} %get-tuple-element.170), channel_id=1, source_target_pairs={{0,1},{1,0},{2,3},{3,2},{4,5},{5,4},{6,7},{7,6}} | collective-permute-start | bytes 2654216 | tf_op jit(solution)/shard_map/ppermute | solution.py:238
  298.3 138.3 %collective-permute-start.28 = (bf16[4,144,768]{2,1,0:T(8,128)(2,1)}, bf16[4,144,768]{2,1,0:T(8,128)(2,1)}, u32[]{:S(2)}, u32[]{:S(2)}) collective-permute-start(bf16[4,144,768]{2,1,0:T(8,128)(2,1)} %get-tuple-element.169), channel_id=1, source_target_pairs={{0,2},{1,3},{2,0},{3,1},{4,6},{5,7},{6,4},{7,5}} | collective-permute-start | bytes 2654216 | tf_op jit(solution)/shard_map/ppermute | solution.py:238
  299.8 138.2 %collective-permute-start.29 = (bf16[4,144,768]{2,1,0:T(8,128)(2,1)}, bf16[4,144,768]{2,1,0:T(8,128)(2,1)}, u32[]{:S(2)}, u32[]{:S(2)}) collective-permute-start(bf16[4,144,768]{2,1,0:T(8,128)(2,1)} %get-tuple-element.168), channel_id=1, source_target_pairs={{0,3},{1,2},{2,1},{3,0},{4,7},{5,6},{6,5},{7,4}} | collective-permute-start | bytes 2654216 | tf_op jit(solution)/shard_map/ppermute | solution.py:238
  299.8 138.8 %collective-permute-start.30 = (bf16[4,144,768]{2,1,0:T(8,128)(2,1)}, bf16[4,144,768]{2,1,0:T(8,128)(2,1)}, u32[]{:S(2)}, u32[]{:S(2)}) collective-permute-start(bf16[4,144,768]{2,1,0:T(8,128)(2,1)} %get-tuple-element.158), channel_id=1, source_target_pairs={{0,1},{1,0},{2,3},{3,2},{4,5},{5,4},{6,7},{7,6}} | collective-permute-start | bytes 2654216 | tf_op jit(solution)/shard_map/ppermute | solution.py:238
  300.5 138.3 %collective-permute-start.31 = (bf16[4,144,768]{2,1,0:T(8,128)(2,1)}, bf16[4,144,768]{2,1,0:T(8,128)(2,1)}, u32[]{:S(2)}, u32[]{:S(2)}) collective-permute-start(bf16[4,144,768]{2,1,0:T(8,128)(2,1)} %get-tuple-element.157), channel_id=1, source_target_pairs={{0,2},{1,3},{2,0},{3,1},{4,6},{5,7},{6,4},{7,5}} | collective-permute-start | bytes 2654216 | tf_op jit(solution)/shard_map/ppermute | solution.py:238
  301.9 138.2 %collective-permute-start.32 = (bf16[4,144,768]{2,1,0:T(8,128)(2,1)S(1)}, bf16[4,144,768]{2,1,0:T(8,128)(2,1)}, u32[]{:S(2)}, u32[]{:S(2)}) collective-permute-start(bf16[4,144,768]{2,1,0:T(8,128)(2,1)S(1)} %get-tuple-element.156), channel_id=1, source_target_pairs={{0,3},{1,2},{2,1},{3,0},{4,7},{5,6},{6,5},{7,4}} | collective-permute-start | bytes 2654216 | tf_op jit(solution)/shard_map/ppermute | solution.py:238
  436.6 138.8 %collective-permute-start.37 = (bf16[2,144,768]{2,1,0:T(8,128)(2,1)}, bf16[2,144,768]{2,1,0:T(8,128)(2,1)}, u32[]{:S(2)}, u32[]{:S(2)}) collective-permute-start(bf16[2,144,768]{2,1,0:T(8,128)(2,1)} %get-tuple-element.155), channel_id=1, source_target_pairs={{0,2},{1,3},{2,0},{3,1},{4,6},{5,7},{6,4},{7,5}} | collective-permute-start | bytes 1327112 | tf_op jit(solution)/shard_map/ppermute | solution.py:238
  438.0 137.4 %collective-permute-start.38 = (bf16[2,144,768]{2,1,0:T(8,128)(2,1)}, bf16[2,144,768]{2,1,0:T(8,128)(2,1)}, u32[]{:S(2)}, u32[]{:S(2)}) collective-permute-start(bf16[2,144,768]{2,1,0:T(8,128)(2,1)} %get-tuple-element.148), channel_id=1, source_target_pairs={{0,3},{1,2},{2,1},{3,0},{4,7},{5,6},{6,5},{7,4}} | collective-permute-start | bytes 1327112 | tf_op jit(solution)/shard_map/ppermute | solution.py:238
  438.6 136.7 %collective-permute-start.39 = (bf16[2,144,768]{2,1,0:T(8,128)(2,1)}, bf16[2,144,768]{2,1,0:T(8,128)(2,1)}, u32[]{:S(2)}, u32[]{:S(2)}) collective-permute-start(bf16[2,144,768]{2,1,0:T(8,128)(2,1)} %get-tuple-element.141), channel_id=1, source_target_pairs={{0,1},{1,0},{2,3},{3,2},{4,5},{5,4},{6,7},{7,6}} | collective-permute-start | bytes 1327112 | tf_op jit(solution)/shard_map/ppermute | solution.py:238
  438.7 136.6 %collective-permute-start.40 = (bf16[2,144,768]{2,1,0:T(8,128)(2,1)}, bf16[2,144,768]{2,1,0:T(8,128)(2,1)}, u32[]{:S(2)}, u32[]{:S(2)}) collective-permute-start(bf16[2,144,768]{2,1,0:T(8,128)(2,1)} %get-tuple-element.147), channel_id=1, source_target_pairs={{0,2},{1,3},{2,0},{3,1},{4,6},{5,7},{6,4},{7,5}} | collective-permute-start | bytes 1327112 | tf_op jit(solution)/shard_map/ppermute | solution.py:238
  440.1 135.3 %collective-permute-start.41 = (bf16[2,144,768]{2,1,0:T(8,128)(2,1)}, bf16[2,144,768]{2,1,0:T(8,128)(2,1)S(1)}, u32[]{:S(2)}, u32[]{:S(2)}) collective-permute-start(bf16[2,144,768]{2,1,0:T(8,128)(2,1)} %get-tuple-element.140), channel_id=1, source_target_pairs={{0,3},{1,2},{2,1},{3,0},{4,7},{5,6},{6,5},{7,4}} | collective-permute-start | bytes 1327112 | tf_op jit(solution)/shard_map/ppermute | solution.py:238
  721.7 141.6 %collective-permute-start.67 = (f32[128,3072]{1,0:T(8,128)S(1)}, f32[128,3072]{1,0:T(8,128)S(1)}, u32[]{:S(2)}, u32[]{:S(2)}) collective-permute-start(f32[128,3072]{1,0:T(8,128)S(1)} %get-tuple-element.189), channel_id=1, source_target_pairs={{0,2},{1,3},{2,0},{3,1},{4,6},{5,7},{6,4},{7,5}} | collective-permute-start | bytes 4718600 | tf_op jit(solution)/shard_map/ppermute | solution.py:238
  739.1 105.3 %collective-permute-start.25 = (bf16[4,144,768]{2,1,0:T(8,128)(2,1)S(1)}, bf16[4,144,768]{2,1,0:T(8,128)(2,1)S(1)}, u32[]{:S(2)}, u32[]{:S(2)}) collective-permute-start(bf16[4,144,768]{2,1,0:T(8,128)(2,1)S(1)} %copy-done.34), channel_id=1, source_target_pairs={{0,2},{1,3},{2,0},{3,1},{4,6},{5,7},{6,4},{7,5}} | collective-permute-start | bytes 2654216 | tf_op jit(solution)/shard_map/ppermute | solution.py:238
  757.0 105.3 %collective-permute-start.26 = (bf16[4,144,768]{2,1,0:T(8,128)(2,1)S(1)}, bf16[4,144,768]{2,1,0:T(8,128)(2,1)S(1)}, u32[]{:S(2)}, u32[]{:S(2)}) collective-permute-start(bf16[4,144,768]{2,1,0:T(8,128)(2,1)S(1)} %copy-done.32), channel_id=1, source_target_pairs={{0,3},{1,2},{2,1},{3,0},{4,7},{5,6},{6,5},{7,4}} | collective-permute-start | bytes 2654216 | tf_op jit(solution)/shard_map/ppermute | solution.py:238
  791.8 78.3 %collective-permute-start.48 = (bf16[4,144,768]{2,1,0:T(8,128)(2,1)S(1)}, bf16[4,144,768]{2,1,0:T(8,128)(2,1)S(1)}, u32[]{:S(2)}, u32[]{:S(2)}) collective-permute-start(bf16[4,144,768]{2,1,0:T(8,128)(2,1)S(1)} %copy-done.27), channel_id=1, source_target_pairs={{0,1},{1,0},{2,3},{3,2},{4,5},{5,4},{6,7},{7,6}} | collective-permute-start | bytes 2654216 | tf_op jit(solution)/shard_map/ppermute | solution.py:238
  797.5 84.9 %collective-permute-start.49 = (bf16[4,144,768]{2,1,0:T(8,128)(2,1)S(1)}, bf16[4,144,768]{2,1,0:T(8,128)(2,1)S(1)}, u32[]{:S(2)}, u32[]{:S(2)}) collective-permute-start(bf16[4,144,768]{2,1,0:T(8,128)(2,1)S(1)} %copy-done.26), channel_id=1, source_target_pairs={{0,2},{1,3},{2,0},{3,1},{4,6},{5,7},{6,4},{7,5}} | collective-permute-start | bytes 2654216 | tf_op jit(solution)/shard_map/ppermute | solution.py:238
  882.4 106.2 %collective-permute-start.70 = (f32[128,3072]{1,0:T(8,128)S(1)}, f32[128,3072]{1,0:T(8,128)S(1)}, u32[]{:S(2)}, u32[]{:S(2)}) collective-permute-start(f32[128,3072]{1,0:T(8,128)S(1)} %get-tuple-element.188), channel_id=1, source_target_pairs={{0,2},{1,3},{2,0},{3,1},{4,6},{5,7},{6,4},{7,5}} | collective-permute-start | bytes 4718600 | tf_op jit(solution)/shard_map/ppermute | solution.py:238
  939.7 84.8 %collective-permute-start.53 = (bf16[4,144,768]{2,1,0:T(8,128)(2,1)S(1)}, bf16[4,144,768]{2,1,0:T(8,128)(2,1)S(1)}, u32[]{:S(2)}, u32[]{:S(2)}) collective-permute-start(bf16[4,144,768]{2,1,0:T(8,128)(2,1)S(1)} %copy-done.20), channel_id=1, source_target_pairs={{0,3},{1,2},{2,1},{3,0},{4,7},{5,6},{6,5},{7,4}} | collective-permute-start | bytes 2654216 | tf_op jit(solution)/shard_map/ppermute | solution.py:238
  987.7 90.6 %collective-permute-start.82 = (f32[512,768]{1,0:T(8,128)S(1)}, f32[512,768]{1,0:T(8,128)S(1)}, u32[]{:S(2)}, u32[]{:S(2)}) collective-permute-start(f32[512,768]{1,0:T(8,128)S(1)} %get-tuple-element.180), channel_id=1, source_target_pairs={{0,2},{1,3},{2,0},{3,1},{4,6},{5,7},{6,4},{7,5}} | collective-permute-start | bytes 4718600 | tf_op jit(solution)/shard_map/ppermute | solution.py:238
  1043.5 88.3 %collective-permute-start.73 = (f32[128,3072]{1,0:T(8,128)S(1)}, f32[128,3072]{1,0:T(8,128)S(1)}, u32[]{:S(2)}, u32[]{:S(2)}) collective-permute-start(f32[128,3072]{1,0:T(8,128)S(1)} %get-tuple-element.185), channel_id=1, source_target_pairs={{0,2},{1,3},{2,0},{3,1},{4,6},{5,7},{6,4},{7,5}} | collective-permute-start | bytes 4718600 | tf_op jit(solution)/shard_map/ppermute | solution.py:238
  1048.3 82.7 %collective-permute-start.55 = (bf16[4,144,768]{2,1,0:T(8,128)(2,1)S(1)}, bf16[4,144,768]{2,1,0:T(8,128)(2,1)S(1)}, u32[]{:S(2)}, u32[]{:S(2)}) collective-permute-start(bf16[4,144,768]{2,1,0:T(8,128)(2,1)S(1)} %copy-done.19), channel_id=1, source_target_pairs={{0,2},{1,3},{2,0},{3,1},{4,6},{5,7},{6,4},{7,5}} | collective-permute-start | bytes 2654216 | tf_op jit(solution)/shard_map/ppermute | solution.py:238
  1050.4 98.4 %collective-permute-start.56 = (bf16[4,144,768]{2,1,0:T(8,128)(2,1)S(1)}, bf16[4,144,768]{2,1,0:T(8,128)(2,1)S(1)}, u32[]{:S(2)}, u32[]{:S(2)}) collective-permute-start(bf16[4,144,768]{2,1,0:T(8,128)(2,1)S(1)} %copy-done.18), channel_id=1, source_target_pairs={{0,3},{1,2},{2,1},{3,0},{4,7},{5,6},{6,5},{7,4}} | collective-permute-start | bytes 2654216 | tf_op jit(solution)/shard_map/ppermute | solution.py:238
  1079.7 79.7 %collective-permute-start.58 = (bf16[2,144,768]{2,1,0:T(8,128)(2,1)S(1)}, bf16[2,144,768]{2,1,0:T(8,128)(2,1)S(1)}, u32[]{:S(2)}, u32[]{:S(2)}) collective-permute-start(bf16[2,144,768]{2,1,0:T(8,128)(2,1)S(1)} %copy-done.36), channel_id=1, source_target_pairs={{0,2},{1,3},{2,0},{3,1},{4,6},{5,7},{6,4},{7,5}} | collective-permute-start | bytes 1327112 | tf_op jit(solution)/shard_map/ppermute | solution.py:238
  1081.7 88.2 %collective-permute-start.64 = (f32[192,576]{1,0:T(8,128)S(1)}, f32[192,576]{1,0:T(8,128)S(1)}, u32[]{:S(2)}, u32[]{:S(2)}) collective-permute-start(f32[192,576]{1,0:T(8,128)S(1)} %dynamic-slice_add_fusion.6), channel_id=1, source_target_pairs={{0,2},{1,3},{2,0},{3,1},{4,6},{5,7},{6,4},{7,5}} | collective-permute-start | bytes 1327112 | tf_op jit(solution)/shard_map/ppermute | solution.py:238
  1131.8 82.1 %collective-permute-start.83 = (f32[512,768]{1,0:T(8,128)S(1)}, f32[512,768]{1,0:T(8,128)}, u32[]{:S(2)}, u32[]{:S(2)}) collective-permute-start(f32[512,768]{1,0:T(8,128)S(1)} %get-tuple-element.127), channel_id=1, source_target_pairs={{0,1},{1,0},{2,3},{3,2},{4,5},{5,4},{6,7},{7,6}} | collective-permute-start | bytes 4718600 | tf_op jit(solution)/shard_map/ppermute | solution.py:238
  (94 other events, 3750.8 us)

commit v2 on v1

v2 whole, which is shorter than its diff:
```python
import functools

import jax
import jax.numpy as jnp
from jax import lax
from jax.experimental import pallas as pl
from jax.experimental.pallas import tpu as pltpu
from jax.sharding import PartitionSpec as P


LN_EPS = 1e-6
GELU_C = 0.7978845608028654
GELU_K = 0.044715
F32 = jnp.float32
BF16 = jnp.bfloat16

CHUNK_SIZES = (2, 4, 6, 4)
PIECE_ROWS = 128
HID_BLOCK = 512
ROW_BLOCK = 48
COL_BLOCK = 256


def gelu_parts(pre):
    sq = pre * pre
    th = jnp.tanh(pre * (GELU_C + (GELU_C * GELU_K) * sq))
    one_plus = 1.0 + th
    inner_slope = pre * (0.5 * GELU_C + (1.5 * GELU_C * GELU_K) * sq)
    return (0.5 * pre) * one_plus, one_plus * (0.5 + inner_slope * (1.0 - th))


def gelu_value(pre):
    sq = pre * pre
    th = jnp.tanh(pre * (GELU_C + (GELU_C * GELU_K) * sq))
    return pre * (0.5 + 0.5 * th)


def gelu_slope(pre):
    return gelu_parts(pre)[1]


def dot(a, b):
    return jnp.dot(a, b, preferred_element_type=F32)


def dot_nt(a, b):
    return lax.dot_general(a, b, (((1,), (1,)), ((), ())), preferred_element_type=F32)


def layer_kernel(first, *refs):
    x_refs, dz_refs = refs[0:4], refs[4:8]
    (ln1_s, ln1_b, ln2_s, ln2_b, b_c1, b_c2, b_t1, b_t2, w_t1, w_t1t, w_t2, w_t2t,
     w_c1, w_c2) = refs[8:22]
    pos = 22
    if not first:
        tok_in, chan_in = refs[pos:pos + 2]
        pos += 2
    z_refs, dx_refs = refs[pos:pos + 4], refs[pos + 4:pos + 8]
    tok_out, chan_out = refs[pos + 8:pos + 10]
    (g_c1, g_c2, g_t1, g_t2, u_s, v_s, vt_s, dz_s, h_s, g_s, x1_s, dv_s, acc_s, dzt_s, stat_s, sem) = refs[pos + 10:]
    accs = (g_t1, g_t2, g_c1, g_c2)
    step = pl.program_id(0)
    rows = x_refs[0].shape[1]
    total_rows = 4 * rows
    chans = u_s.shape[1]
    hid = w_c1.shape[1]

    last_step = step == pl.num_programs(0) - 1

    def load_copies():
        srcs = (tok_in.at[0], tok_in.at[1], chan_in.at[0], chan_in.at[1])
        return [pltpu.make_async_copy(src, acc, sem.at[i]) for i, (src, acc) in enumerate(zip(srcs, accs))]

    def store_copy(i):
        dst = (tok_out, chan_out)[i // 2].at[i % 2]
        return pltpu.make_async_copy(accs[i], dst, sem.at[4 + i])

    @pl.when(step == 0)
    def _():
        if first:
            for acc in accs:
                acc[...] = jnp.zeros_like(acc)
        else:
            for cp in load_copies():
                cp.start()

    def widen(stat):
        return jnp.concatenate([stat] * (chans // 128), axis=1)

    def norm(val, scale, shift, mean_at, inv_at):
        mean = jnp.mean(val, axis=-1, keepdims=True)
        cen = val - mean
        var = jnp.mean(cen * cen, axis=-1, keepdims=True)
        inv = lax.rsqrt(var + LN_EPS)
        mean_at[...] = jnp.broadcast_to(mean, mean_at.shape)
        inv_at[...] = jnp.broadcast_to(inv, inv_at.shape)
        return (cen * inv * scale + shift).astype(BF16)

    def norm_grad(val, grad, scale, mean, inv):
        inv = widen(inv)
        hat = (val - widen(mean)) * inv
        gs = grad * scale
        m1 = jnp.mean(gs, axis=-1, keepdims=True)
        m2 = jnp.mean(gs * hat, axis=-1, keepdims=True)
        return (inv * (gs - m1 - hat * m2)).astype(BF16)

    per_block = rows // ROW_BLOCK

    for k in range(4):
        def ln1_step(i, carry, k=k):
            r = pl.multiple_of(i * ROW_BLOCK, 16)
            dst = pl.ds(k * rows + r, ROW_BLOCK)
            u_s[dst, :] = norm(x_refs[k][0, pl.ds(r, ROW_BLOCK), :].astype(F32), ln1_s[...], ln1_b[...],
                               stat_s.at[0, dst], stat_s.at[1, dst])
            dz_s[dst, :] = dz_refs[k][0, pl.ds(r, ROW_BLOCK), :]
            return carry

        lax.fori_loop(0, per_block, ln1_step, 0, unroll=True)

    for n in range(chans // COL_BLOCK):
        cols = slice(n * COL_BLOCK, (n + 1) * COL_BLOCK)
        h = (dot(w_t1t[...], u_s[:, cols]) + b_t1[...]).astype(BF16)
        h_s[:, cols] = h
        g = gelu_value(h.astype(F32)).astype(BF16)
        g_s[:, cols] = g
        t = (dot(w_t2t[...], g) + b_t2[...]).astype(BF16)
        for k in range(4):
            part = slice(k * rows, (k + 1) * rows)
            x1_s[part, cols] = (x_refs[k][0, :, cols].astype(F32) + t[part].astype(F32)).astype(BF16)

    def ln2_step(i, carry):
        r = pl.ds(pl.multiple_of(i * ROW_BLOCK, 16), ROW_BLOCK)
        x1 = x1_s[r, :].astype(F32)
        acc_s[r, :] = x1 + b_c2[...]
        v_s[r, :] = norm(x1, ln2_s[...], ln2_b[...], stat_s.at[2, r], stat_s.at[3, r])
        return carry

    lax.fori_loop(0, total_rows // ROW_BLOCK, ln2_step, 0, unroll=True)

    vt_s[...] = v_s[...].T
    dzt_s[...] = dz_s[...].T
    dv_s[...] = jnp.zeros_like(dv_s)

    if not first:
        @pl.when(step == 0)
        def _():
            for cp in load_copies():
                cp.wait()

    def hid_step(j, carry):
        cols = pl.ds(pl.multiple_of(j * HID_BLOCK, HID_BLOCK), HID_BLOCK)
        v = v_s[...]
        dz = dz_s[...]
        a = (dot(v, w_c1[:, cols]) + b_c1[:, cols]).astype(BF16)
        q32, slope = gelu_parts(a.astype(F32))
        q = q32.astype(BF16)
        dq = dot_nt(dz, w_c2[cols, :]).astype(BF16)
        da = (dq.astype(F32) * slope).astype(BF16)
        acc_s[...] += dot(q, w_c2[cols, :])
        dv_s[...] += dot_nt(da, w_c1[:, cols])
        g_c1[:, cols] += dot(vt_s[...], da)
        g_c2[:, cols] += dot(dzt_s[...], q)
        return carry

    lax.fori_loop(0, hid // HID_BLOCK, hid_step, 0)

    @pl.when(last_step)
    def _():
        store_copy(2).start()
        store_copy(3).start()

    for k in range(4):
        def ln2_back(i, carry, k=k):
            r = pl.multiple_of(i * ROW_BLOCK, 16)
            src = pl.ds(k * rows + r, ROW_BLOCK)
            x1 = x1_s[src, :].astype(F32)
            z_refs[k][0, pl.ds(r, ROW_BLOCK), :] = acc_s[src, :].astype(BF16)
            dln = norm_grad(x1, dv_s[src, :].astype(BF16).astype(F32), ln2_s[...], stat_s[2, src], stat_s[3, src])
            v_s[src, :] = (dz_s[src, :].astype(F32) + dln.astype(F32)).astype(BF16)
            return carry

        lax.fori_loop(0, per_block, ln2_back, 0, unroll=True)

    g_t2[...] += dot_nt(v_s[...], g_s[...])
    for n in range(chans // COL_BLOCK):
        cols = slice(n * COL_BLOCK, (n + 1) * COL_BLOCK)
        dg = dot(w_t2[...], v_s[:, cols]).astype(BF16)
        dh = (dg.astype(F32) * gelu_slope(h_s[:, cols].astype(F32))).astype(BF16)
        g_s[:, cols] = dh
        dv_s[:, cols] = dot(w_t1[...], dh)
    g_t1[...] += dot_nt(u_s[...], g_s[...])

    for k in range(4):
        def ln1_back(i, carry, k=k):
            r = pl.multiple_of(i * ROW_BLOCK, 16)
            src = pl.ds(k * rows + r, ROW_BLOCK)
            x = x_refs[k][0, pl.ds(r, ROW_BLOCK), :].astype(F32)
            dln = norm_grad(x, dv_s[src, :].astype(BF16).astype(F32), ln1_s[...], stat_s[0, src], stat_s[1, src])
            dx_refs[k][0, pl.ds(r, ROW_BLOCK), :] = (v_s[src, :].astype(F32) + dln.astype(F32)).astype(BF16)
            return carry

        lax.fori_loop(0, per_block, ln1_back, 0, unroll=True)

    @pl.when(last_step)
    def _():
        store_copy(0).start()
        store_copy(1).start()
        for i in range(4):
            store_copy(i).wait()


def layer_call(xs, dzs, params, accs):
    images, rows, chans = xs[0].shape
    w_t1, w_c1 = params[8], params[12]
    total_rows, tok_hid = w_t1.shape
    hid = w_c1.shape[1]
    first = accs is None
    block = pl.BlockSpec((1, rows, chans), lambda i: (i, 0, 0))
    whole = pl.BlockSpec(memory_space=pltpu.VMEM)
    anywhere = pl.BlockSpec(memory_space=pl.ANY)
    tok_shape, chan_shape = (total_rows, tok_hid), (chans, hid)
    act = jax.ShapeDtypeStruct((images, rows, chans), BF16)
    out_shape = [act] * 8 + [jax.ShapeDtypeStruct((2,) + tok_shape, F32), jax.ShapeDtypeStruct((2,) + chan_shape, F32)]
    n_in = 8 + len(params)
    acc_args = () if first else tuple(accs)
    flops = images * (12 * total_rows * chans * hid + 12 * total_rows * chans * tok_hid)
    return pl.pallas_call(
        functools.partial(layer_kernel, first),
        grid=(images,),
        in_specs=[block] * 8 + [whole] * len(params) + [anywhere] * len(acc_args),
        out_specs=[block] * 8 + [anywhere] * 2,
        out_shape=out_shape,
        scratch_shapes=[
            pltpu.VMEM(chan_shape, F32), pltpu.VMEM(chan_shape, F32),
            pltpu.VMEM(tok_shape, F32), pltpu.VMEM(tok_shape, F32),
            pltpu.VMEM((total_rows, chans), BF16), pltpu.VMEM((total_rows, chans), BF16),
            pltpu.VMEM((chans, total_rows), BF16), pltpu.VMEM((total_rows, chans), BF16),
            pltpu.VMEM((tok_hid, chans), BF16), pltpu.VMEM((tok_hid, chans), BF16),
            pltpu.VMEM((total_rows, chans), BF16),
            pltpu.VMEM((total_rows, chans), F32), pltpu.VMEM((total_rows, chans), F32),
            pltpu.VMEM((chans, total_rows), BF16),
            pltpu.VMEM((4, total_rows, 128), F32),
            pltpu.SemaphoreType.DMA((8,)),
        ],
        input_output_aliases={} if first else {n_in: 8, n_in + 1: 9},
        compiler_params=pltpu.CompilerParams(
            dimension_semantics=("arbitrary",), vmem_limit_bytes=66_000_000),
        cost_estimate=pl.CostEstimate(flops=flops, bytes_accessed=60_000_000, transcendentals=0),
    )(*xs, *dzs, *params, *acc_args)


def place_kernel(core_ref, full_ref, peer_ref, *refs):
    out1_ref, out2_ref = refs[-2:]
    is_first = core_ref[0] == 0
    full, peer = full_ref[...], peer_ref[...]
    out1_ref[...] = jnp.where(is_first, full, peer)
    out2_ref[...] = jnp.where(is_first, peer, full).T


def place_piece(core, full, peer, piece, bufs, chans):
    size, hid = full.shape
    width = 512
    part = pl.BlockSpec((size, width), lambda j, core_ref: (0, j))
    anywhere = pl.BlockSpec(memory_space=pl.ANY)
    bufs = () if bufs is None else tuple(bufs)
    return pl.pallas_call(
        place_kernel,
        grid_spec=pltpu.PrefetchScalarGridSpec(
            num_scalar_prefetch=1, grid=(hid // width,),
            in_specs=[part, part] + [anywhere] * len(bufs),
            out_specs=[pl.BlockSpec((size, width), lambda j, core_ref: (piece, j)),
                       pl.BlockSpec((width, size), lambda j, core_ref: (j, piece))]),
        out_shape=[jax.ShapeDtypeStruct((chans, hid), F32), jax.ShapeDtypeStruct((hid, chans), F32)],
        input_output_aliases={3 + i: i for i in range(len(bufs))},
        compiler_params=pltpu.CompilerParams(vmem_limit_bytes=16_000_000),
        cost_estimate=pl.CostEstimate(flops=0, bytes_accessed=4 * 4 * size * hid, transcendentals=0),
    )(core, full, peer, *bufs)


def solution(mesh):
    act_spec = P("data", "seq", None)
    part_spec = P("data", None)
    spec_in = (act_spec, act_spec) + (P(),) * 12
    spec_out = (act_spec, act_spec, part_spec, part_spec, part_spec, part_spec)
    ranks = mesh.shape["seq"]

    def hop(val, dist):
        return lax.ppermute(val, "seq", [(i, i ^ dist) for i in range(ranks)])

    def device_body(act_loc, grad_loc, ln1_scale, ln1_shift, w_tok1, b_tok1, w_tok2, b_tok2,
                    ln2_scale, ln2_shift, w_chan1, b_chan1, w_chan2, b_chan2):
        me = lax.axis_index("seq")
        core = me % 2
        images, rows, chans = act_loc.shape
        own = images // ranks

        def permute_blocks(arr, axis):
            parts = [lax.dynamic_slice_in_dim(arr, (me ^ d) * rows, rows, axis) for d in range(ranks)]
            return jnp.concatenate(parts, axis)

        w_t1 = permute_blocks(w_tok1, 0)
        w_t2 = permute_blocks(w_tok2, 1)
        b_t2 = permute_blocks(b_tok2, 0)
        params = (ln1_scale[None], ln1_shift[None], ln2_scale[None], ln2_shift[None], b_chan1[None], b_chan2[None],
                  b_tok1[:, None], b_t2[:, None], w_t1, w_t1.T, w_t2, w_t2.T,
                  w_chan1, w_chan2)

        def fetch(arr, start, size):
            blocks = []
            for d in range(ranks):
                piece = lax.dynamic_slice_in_dim(arr, (me ^ d) * own + start, size, 0)
                blocks.append(piece if d == 0 else hop(piece, d))
            return blocks

        starts = [sum(CHUNK_SIZES[:c]) for c in range(len(CHUNK_SIZES))]
        ins = [(fetch(act_loc, s, n), fetch(grad_loc, s, n))
               for s, n in zip(starts, CHUNK_SIZES)]
        accs = None
        back = []
        for c, offset in enumerate(starts):
            outs = layer_call(ins[c][0], ins[c][1], params, accs)
            accs = outs[8:]
            for d in range(ranks):
                z, dx = outs[d], outs[4 + d]
                if d:
                    z, dx = hop(z, d), hop(dx, d)
                back.append(((me ^ d) * own + offset, z, dx))

        tok, chan = accs
        tok = permute_blocks(tok, 1)

        def pair_sum(stack, at, size):
            width = stack.shape[2]
            mine = lax.dynamic_slice(stack, (core, at, 0), (1, size, width))[0]
            other = lax.dynamic_slice(stack, (1 - core, at, 0), (1, size, width))[0]
            got = hop(other, 1)
            return mine + got

        pieces = chans // PIECE_ROWS
        pairs = [pair_sum(chan, p * PIECE_ROWS, PIECE_ROWS) for p in range(pieces)]
        tok_pair = pair_sum(tok, 0, tok.shape[1])

        blank = jnp.zeros((), BF16)
        blank, pairs, tok_pair = lax.optimization_barrier((blank, pairs, tok_pair))
        act_out = jnp.broadcast_to(blank, act_loc.shape)
        grad_in = jnp.broadcast_to(blank, act_loc.shape)
        for start, z, dx in back:
            act_out = lax.dynamic_update_slice_in_dim(act_out, z, start, 0)
            grad_in = lax.dynamic_update_slice_in_dim(grad_in, dx, start, 0)

        bufs = None
        for p, pair in enumerate(pairs):
            got = hop(pair, 2)
            full = pair + got
            peer = hop(full, 1)
            bufs = place_piece(core[None], full, peer, p, bufs, chans)
        g_c1, g_c2 = bufs
        full = tok_pair + hop(tok_pair, 2)
        peer = hop(full, 1)
        g_t1 = jnp.where(core == 0, full, peer)
        g_t2 = jnp.where(core == 0, peer, full).T
        return act_out, grad_in, g_t1, g_t2, g_c1, g_c2

    return jax.shard_map(device_body, mesh=mesh, in_specs=spec_in, out_specs=spec_out, check_vma=False)
```

time: 1220 us -> 1120 us (0.918)
  Pallas kernels: 555 us -> 502 us
  waiting for transfers between devices: 459 us -> 428 us
  local copies, waits for them, and re-layouts: 125 us -> 106 us
    pallas_call x5 -> x4, Pallas kernels: 555 us -> 484 us  [layer_call(): pl.pallas_call(functools.partial(layer_kernel, first), grid=(images,), in...]
    ppermute x84 -> x69, waiting for transfers between devices: 459 us -> 428 us  [hop(): return lax.ppermute(val, 'seq', [(i, i ^ dist) for i in range(ranks)])]
    dynamic_update_slice x9 -> x0, local copies, waits for them, and re-layouts: 19.7 us -> none  [the longest x8 15.5 us: group_sum(): out = lax.dynamic_update_slice_in_dim(out, peer, other_at, 0)]
    pallas_call x0 -> x6, Pallas kernels: none -> 17.3 us  [place_piece(): pl.pallas_call(place_kernel, grid_spec=pltpu.PrefetchScalarGridSpec(num_s...]
    add x7 -> x9, other arithmetic: 11.7 us -> 24.4 us  [the longest x2 12.9 us: pair_sum(): return mine + got]
    another operation x2 -> x0, local copies, waits for them, and re-layouts: 12.4 us -> none
    ppermute x84 -> x69, starting transfers between devices: 53.5 us -> 46 us  [hop(): return lax.ppermute(val, 'seq', [(i, i ^ dist) for i in range(ranks)])]
    dynamic_slice x4 -> x6, local copies, waits for them, and re-layouts: 22.9 us -> 26.9 us  [fetch(): piece = lax.dynamic_slice_in_dim(arr, (me ^ d) * own + start, size, 0)]
  transfers between devices with their start and end apart: 84 -> 69, of which waited for: 24 -> 20; matrix products, arithmetic and copies ran while one was open for 12% -> 12% of each run, Pallas kernels for 39% -> 45%
where the time goes in v2:
time: 1120 us; the launch traced here: 1110 us
  Pallas kernels  502 us (45%)
  waiting for transfers between devices  428 us (38%)
  local copies, waits for them, and re-layouts  106 us (9%)
  starting transfers between devices  46 us (4%)
  other arithmetic  28.3 us (3%)
    pallas_call x4, Pallas kernels, layer_call(): pl.pallas_call(functools.partial(layer_kernel, first), grid=(images,), in...  484 us
    ppermute x69, waiting for transfers between devices, hop(): return lax.ppermute(val, 'seq', [(i, i ^ dist) for i in range(ranks)])  428 us
    ppermute x69, starting transfers between devices, hop(): return lax.ppermute(val, 'seq', [(i, i ^ dist) for i in range(ranks)])  46 us
    dynamic_slice x6, local copies, waits for them, and re-layouts, fetch(): piece = lax.dynamic_slice_in_dim(arr, (me ^ d) * own + start, size, 0)  26.9 us
    dynamic_update_slice x16, local copies, waits for them, and re-layouts, device_body(): grad_in = lax.dynamic_update_slice_in_dim(grad_in, dx, start, 0)  24.1 us
    dynamic_update_slice x15, local copies, waits for them, and re-layouts, device_body(): act_out = lax.dynamic_update_slice_in_dim(act_out, z, start, 0)  24.1 us
  transfers between devices with their start and end apart: 69, of which 20 were waited for; matrix products, arithmetic and copies ran while one was open for 12% of the time, Pallas kernels for 45%

profile of v2, /device:TPU:0, one launch (start us, length us, event | category | flops | bytes accessed | tf_op | source)
XLA Modules:
  0.0 1111.7 jit_solution(12799336700003542869)
XLA Ops:
  13.4 5.0 constant_dynamic-slice_fusion.24
  19.1 5.7 constant_dynamic-slice_fusion.16
  29.5 4.9 constant_dynamic-slice_fusion.20
  45.6 6.0 constant_dynamic-slice_fusion.12
  51.6 32.5 %collective-permute-done.23.refs_7_ = bf16[2,144,768]{2,1,0:T(8,128)(2,1)} collective-permute-done((bf16[2,144,768]{2,1,0:T(8,128)(2,1)S(1)}, bf16[2,144,768]{2,1,0:T(8,128)(2,1)}, u32[]{:S(2)}, u32[]{:S(2)}) %collective-permute-start.23) | collective-permute-done | bytes 442400 | tf_op jit(solution)/shard_map/ppermute | solution.py:288
  87.5 67.8 %shard_map.181 = (bf16[2,144,768]{2,1,0:T(8,128)(2,1)}, bf16[2,144,768]{2,1,0:T(8,128)(2,1)}, bf16[2,144,768]{2,1,0:T(8,128)(2,1)}, bf16[2,144,768]{2,1,0:T(8,12...) custom-call(bf16[2,144,768]{2,1,0:T(8,128)(2,1)} %get-tuple-element., ...), custom_call_target="tpu_custom_call" | custom-call | flops 36691771392 | bytes 60000000 | tf_op jit(solution)/shard_map/pallas_call | solution.py:227
  159.1 120.9 %shard_map.182 = (bf16[4,144,768]{2,1,0:T(8,128)(2,1)}, bf16[4,144,768]{2,1,0:T(8,128)(2,1)}, bf16[4,144,768]{2,1,0:T(8,128)(2,1)}, bf16[4,144,768]{2,1,0:T(8,12...) custom-call(bf16[4,144,768]{2,1,0:T(8,128)(2,1)} %get-tuple-element., ...), custom_call_target="tpu_custom_call", output_to_operand_aliasing={{8}: (22, {}), {9}: (23, {})} | custom-call | flops 73383542784 | bytes 60000000 | tf_op jit(solution)/shard_map/pallas_call | solution.py:227
  283.0 174.4 %shard_map.183 = (bf16[6,144,768]{2,1,0:T(8,128)(2,1)}, bf16[6,144,768]{2,1,0:T(8,128)(2,1)}, bf16[6,144,768]{2,1,0:T(8,128)(2,1)}, bf16[6,144,768]{2,1,0:T(8,12...) custom-call(bf16[6,144,768]{2,1,0:T(8,128)(2,1)} %get-tuple-element., ...), custom_call_target="tpu_custom_call", output_to_operand_aliasing={{8}: (22, {}), {9}: (23, {})} | custom-call | flops 110075314176 | bytes 60000000 | tf_op jit(solution)/shard_map/pallas_call | solution.py:227
  461.1 121.1 %shard_map.184 = (bf16[4,144,768]{2,1,0:T(8,128)(2,1)}, bf16[4,144,768]{2,1,0:T(8,128)(2,1)}, bf16[4,144,768]{2,1,0:T(8,128)(2,1)}, bf16[4,144,768]{2,1,0:T(8,12...) custom-call(bf16[4,144,768]{2,1,0:T(8,128)(2,1)} %get-tuple-element., ...), custom_call_target="tpu_custom_call", output_to_operand_aliasing={{8}: (22, {}), {9}: (23, {})} | custom-call | flops 73383542784 | bytes 60000000 | tf_op jit(solution)/shard_map/pallas_call | solution.py:227
  586.3 9.2 collective-permute-done.32
  595.5 7.9 collective-permute-done.33
  606.5 7.0 dynamic-slice_bitcast_fusion
  613.5 8.9 collective-permute-done.36
  624.7 18.2 %collective-permute-done.47 = bf16[4,144,768]{2,1,0:T(8,128)(2,1)S(1)} collective-permute-done((bf16[4,144,768]{2,1,0:T(8,128)(2,1)}, bf16[4,144,768]{2,1,0:T(8,128)(2,1)S(1)}, u32[]{:S(2)}, u32[]{:S(2)}) %collective-permute-start.47) | collective-permute-done | bytes 884768 | tf_op jit(solution)/shard_map/ppermute | solution.py:288
  643.4 16.8 %collective-permute-done.48 = bf16[4,144,768]{2,1,0:T(8,128)(2,1)S(1)} collective-permute-done((bf16[4,144,768]{2,1,0:T(8,128)(2,1)}, bf16[4,144,768]{2,1,0:T(8,128)(2,1)S(1)}, u32[]{:S(2)}, u32[]{:S(2)}) %collective-permute-start.48) | collective-permute-done | bytes 884768 | tf_op jit(solution)/shard_map/ppermute | solution.py:288
  663.3 17.5 %collective-permute-done.41 = bf16[4,144,768]{2,1,0:T(8,128)(2,1)S(1)} collective-permute-done((bf16[4,144,768]{2,1,0:T(8,128)(2,1)S(1)}, bf16[4,144,768]{2,1,0:T(8,128)(2,1)S(1)}, u32[]{:S(2)}, u32[]{:S(2)}) %collective-permute-start.41) | collective-permute-done | bytes 884768 | tf_op jit(solution)/shard_map/ppermute | solution.py:288
  680.8 17.4 %collective-permute-done.42 = bf16[4,144,768]{2,1,0:T(8,128)(2,1)S(1)} collective-permute-done((bf16[4,144,768]{2,1,0:T(8,128)(2,1)S(1)}, bf16[4,144,768]{2,1,0:T(8,128)(2,1)S(1)}, u32[]{:S(2)}, u32[]{:S(2)}) %collective-permute-start.42) | collective-permute-done | bytes 884768 | tf_op jit(solution)/shard_map/ppermute | solution.py:288
  707.2 10.8 bitcast_add_fusion
  718.0 63.5 %collective-permute-done.53 = bf16[4,144,768]{2,1,0:T(8,128)(2,1)} collective-permute-done((bf16[4,144,768]{2,1,0:T(8,128)(2,1)}, bf16[4,144,768]{2,1,0:T(8,128)(2,1)}, u32[]{:S(2)}, u32[]{:S(2)}) %collective-permute-start.53) | collective-permute-done | bytes 884768 | tf_op jit(solution)/shard_map/ppermute | solution.py:288
  786.1 6.2 broadcast_in_dim.44.clone
  794.1 43.9 %collective-permute-done.55 = f32[576,384]{1,0:T(8,128)} collective-permute-done((f32[576,384]{1,0:T(8,128)}, f32[576,384]{1,0:T(8,128)}, u32[]{:S(2)}, u32[]{:S(2)}) %collective-permute-start.55) | collective-permute-done | bytes 884768 | tf_op jit(solution)/shard_map/ppermute | solution.py:288
  840.0 6.2 broadcast_in_dim.44.clone.1
  864.0 7.7 collective-permute-done.57
  874.8 30.6 %collective-permute-done.59 = f32[128,3072]{1,0:T(8,128)} collective-permute-done((f32[128,3072]{1,0:T(8,128)}, f32[128,3072]{1,0:T(8,128)}, u32[]{:S(2)}, u32[]{:S(2)}) %collective-permute-start.59) | collective-permute-done | bytes 1572896 | tf_op jit(solution)/shard_map/ppermute | solution.py:288
  906.0 33.1 %collective-permute-done.61 = f32[128,3072]{1,0:T(8,128)} collective-permute-done((f32[128,3072]{1,0:T(8,128)}, f32[128,3072]{1,0:T(8,128)}, u32[]{:S(2)}, u32[]{:S(2)}) %collective-permute-start.61) | collective-permute-done | bytes 1572896 | tf_op jit(solution)/shard_map/ppermute | solution.py:288
  943.3 29.5 %collective-permute-done.63 = f32[128,3072]{1,0:T(8,128)} collective-permute-done((f32[128,3072]{1,0:T(8,128)S(1)}, f32[128,3072]{1,0:T(8,128)}, u32[]{:S(2)}, u32[]{:S(2)}) %collective-permute-start.63) | collective-permute-done | bytes 1572896 | tf_op jit(solution)/shard_map/ppermute | solution.py:288
  972.8 33.7 %collective-permute-done.65 = f32[128,3072]{1,0:T(8,128)} collective-permute-done((f32[128,3072]{1,0:T(8,128)S(1)}, f32[128,3072]{1,0:T(8,128)}, u32[]{:S(2)}, u32[]{:S(2)}) %collective-permute-start.65) | collective-permute-done | bytes 1572896 | tf_op jit(solution)/shard_map/ppermute | solution.py:288
  1028.4 50.8 %collective-permute-done.54 = bf16[4,144,768]{2,1,0:T(8,128)(2,1)S(1)} collective-permute-done((bf16[4,144,768]{2,1,0:T(8,128)(2,1)S(1)}, bf16[4,144,768]{2,1,0:T(8,128)(2,1)S(1)}, u32[]{:S(2)}, u32[]{:S(2)}) %collective-permute-start.54) | collective-permute-done | bytes 884768 | tf_op jit(solution)/shard_map/ppermute | solution.py:288
  1097.0 2.9 shard_map.186
  1099.9 2.9 shard_map.187
  1102.8 2.9 shard_map.188
  1105.7 2.9 shard_map.189
  (279 shorter events, 141.4 us)
Async XLA Ops:
  84.1 74.0 %collective-permute-start.6 = (bf16[6,144,768]{2,1,0:T(8,128)(2,1)}, bf16[6,144,768]{2,1,0:T(8,128)(2,1)}, u32[]{:S(2)}, u32[]{:S(2)}) collective-permute-start(bf16[6,144,768]{2,1,0:T(8,128)(2,1)} %get-tuple-element.168), channel_id=1, source_target_pairs={{0,1},{1,0},{2,3},{3,2},{4,5},{5,4},{6,7},{7,6}} | collective-permute-start | bytes 3981320 | tf_op jit(solution)/shard_map/ppermute | solution.py:288
  155.3 124.8 %collective-permute-start.7 = (bf16[6,144,768]{2,1,0:T(8,128)(2,1)}, bf16[6,144,768]{2,1,0:T(8,128)(2,1)}, u32[]{:S(2)}, u32[]{:S(2)}) collective-permute-start(bf16[6,144,768]{2,1,0:T(8,128)(2,1)} %get-tuple-element.167), channel_id=1, source_target_pairs={{0,2},{1,3},{2,0},{3,1},{4,6},{5,7},{6,4},{7,5}} | collective-permute-start | bytes 3981320 | tf_op jit(solution)/shard_map/ppermute | solution.py:288
  155.9 124.9 %collective-permute-start.8 = (bf16[6,144,768]{2,1,0:T(8,128)(2,1)}, bf16[6,144,768]{2,1,0:T(8,128)(2,1)}, u32[]{:S(2)}, u32[]{:S(2)}) collective-permute-start(bf16[6,144,768]{2,1,0:T(8,128)(2,1)} %get-tuple-element.166), channel_id=1, source_target_pairs={{0,3},{1,2},{2,1},{3,0},{4,7},{5,6},{6,5},{7,4}} | collective-permute-start | bytes 3981320 | tf_op jit(solution)/shard_map/ppermute | solution.py:288
  157.3 123.5 %collective-permute-start.9 = (bf16[6,144,768]{2,1,0:T(8,128)(2,1)}, bf16[6,144,768]{2,1,0:T(8,128)(2,1)}, u32[]{:S(2)}, u32[]{:S(2)}) collective-permute-start(bf16[6,144,768]{2,1,0:T(8,128)(2,1)} %get-tuple-element.164), channel_id=1, source_target_pairs={{0,1},{1,0},{2,3},{3,2},{4,5},{5,4},{6,7},{7,6}} | collective-permute-start | bytes 3981320 | tf_op jit(solution)/shard_map/ppermute | solution.py:288
  157.5 124.8 %collective-permute-start.10 = (bf16[6,144,768]{2,1,0:T(8,128)(2,1)}, bf16[6,144,768]{2,1,0:T(8,128)(2,1)}, u32[]{:S(2)}, u32[]{:S(2)}) collective-permute-start(bf16[6,144,768]{2,1,0:T(8,128)(2,1)} %get-tuple-element.163), channel_id=1, source_target_pairs={{0,2},{1,3},{2,0},{3,1},{4,6},{5,7},{6,4},{7,5}} | collective-permute-start | bytes 3981320 | tf_op jit(solution)/shard_map/ppermute | solution.py:288
  158.1 124.6 %collective-permute-start.11 = (bf16[6,144,768]{2,1,0:T(8,128)(2,1)}, bf16[6,144,768]{2,1,0:T(8,128)(2,1)}, u32[]{:S(2)}, u32[]{:S(2)}) collective-permute-start(bf16[6,144,768]{2,1,0:T(8,128)(2,1)} %get-tuple-element.162), channel_id=1, source_target_pairs={{0,3},{1,2},{2,1},{3,0},{4,7},{5,6},{6,5},{7,4}} | collective-permute-start | bytes 3981320 | tf_op jit(solution)/shard_map/ppermute | solution.py:288
  280.1 177.3 %collective-permute-start.2 = (bf16[4,144,768]{2,1,0:T(8,128)(2,1)S(1)}, bf16[4,144,768]{2,1,0:T(8,128)(2,1)}, u32[]{:S(2)}, u32[]{:S(2)}) collective-permute-start(bf16[4,144,768]{2,1,0:T(8,128)(2,1)S(1)} %get-tuple-element.158), channel_id=1, source_target_pairs={{0,3},{1,2},{2,1},{3,0},{4,7},{5,6},{6,5},{7,4}} | collective-permute-start | bytes 2654216 | tf_op jit(solution)/shard_map/ppermute | solution.py:288
  280.8 178.1 %collective-permute-start.3 = (bf16[4,144,768]{2,1,0:T(8,128)(2,1)}, bf16[4,144,768]{2,1,0:T(8,128)(2,1)}, u32[]{:S(2)}, u32[]{:S(2)}) collective-permute-start(bf16[4,144,768]{2,1,0:T(8,128)(2,1)} %get-tuple-element.152), channel_id=1, source_target_pairs={{0,1},{1,0},{2,3},{3,2},{4,5},{5,4},{6,7},{7,6}} | collective-permute-start | bytes 2654216 | tf_op jit(solution)/shard_map/ppermute | solution.py:288
  280.8 178.1 %collective-permute-start.4 = (bf16[4,144,768]{2,1,0:T(8,128)(2,1)}, bf16[4,144,768]{2,1,0:T(8,128)(2,1)}, u32[]{:S(2)}, u32[]{:S(2)}) collective-permute-start(bf16[4,144,768]{2,1,0:T(8,128)(2,1)} %get-tuple-element.151), channel_id=1, source_target_pairs={{0,2},{1,3},{2,0},{3,1},{4,6},{5,7},{6,4},{7,5}} | collective-permute-start | bytes 2654216 | tf_op jit(solution)/shard_map/ppermute | solution.py:288
  282.3 177.2 %collective-permute-start.5 = (bf16[4,144,768]{2,1,0:T(8,128)(2,1)}, bf16[4,144,768]{2,1,0:T(8,128)(2,1)}, u32[]{:S(2)}, u32[]{:S(2)}) collective-permute-start(bf16[4,144,768]{2,1,0:T(8,128)(2,1)} %get-tuple-element.150), channel_id=1, source_target_pairs={{0,3},{1,2},{2,1},{3,0},{4,7},{5,6},{6,5},{7,4}} | collective-permute-start | bytes 2654216 | tf_op jit(solution)/shard_map/ppermute | solution.py:288
  282.7 176.9 %collective-permute-start.43 = (bf16[2,144,768]{2,1,0:T(8,128)(2,1)}, bf16[2,144,768]{2,1,0:T(8,128)(2,1)}, u32[]{:S(2)}, u32[]{:S(2)}) collective-permute-start(bf16[2,144,768]{2,1,0:T(8,128)(2,1)} %get-tuple-element.92), channel_id=1, source_target_pairs={{0,1},{1,0},{2,3},{3,2},{4,5},{5,4},{6,7},{7,6}} | collective-permute-start | bytes 1327112 | tf_op jit(solution)/shard_map/ppermute | solution.py:288
  457.4 124.8 %collective-permute-start.44 = (bf16[2,144,768]{2,1,0:T(8,128)(2,1)}, bf16[2,144,768]{2,1,0:T(8,128)(2,1)}, u32[]{:S(2)}, u32[]{:S(2)}) collective-permute-start(bf16[2,144,768]{2,1,0:T(8,128)(2,1)} %get-tuple-element.93), channel_id=1, source_target_pairs={{0,2},{1,3},{2,0},{3,1},{4,6},{5,7},{6,4},{7,5}} | collective-permute-start | bytes 1327112 | tf_op jit(solution)/shard_map/ppermute | solution.py:288
  458.9 123.9 %collective-permute-start.45 = (bf16[2,144,768]{2,1,0:T(8,128)(2,1)}, bf16[2,144,768]{2,1,0:T(8,128)(2,1)}, u32[]{:S(2)}, u32[]{:S(2)}) collective-permute-start(bf16[2,144,768]{2,1,0:T(8,128)(2,1)} %get-tuple-element.94), channel_id=1, source_target_pairs={{0,3},{1,2},{2,1},{3,0},{4,7},{5,6},{6,5},{7,4}} | collective-permute-start | bytes 1327112 | tf_op jit(solution)/shard_map/ppermute | solution.py:288
  459.0 124.8 %collective-permute-start.31 = (bf16[2,144,768]{2,1,0:T(8,128)(2,1)}, bf16[2,144,768]{2,1,0:T(8,128)(2,1)}, u32[]{:S(2)}, u32[]{:S(2)}) collective-permute-start(bf16[2,144,768]{2,1,0:T(8,128)(2,1)} %get-tuple-element.76), channel_id=1, source_target_pairs={{0,1},{1,0},{2,3},{3,2},{4,5},{5,4},{6,7},{7,6}} | collective-permute-start | bytes 1327112 | tf_op jit(solution)/shard_map/ppermute | solution.py:288
  459.6 145.0 %collective-permute-start.34 = (bf16[4,144,768]{2,1,0:T(8,128)(2,1)}, bf16[4,144,768]{2,1,0:T(8,128)(2,1)S(1)}, u32[]{:S(2)}, u32[]{:S(2)}) collective-permute-start(bf16[4,144,768]{2,1,0:T(8,128)(2,1)} %get-tuple-element.80), channel_id=1, source_target_pairs={{0,1},{1,0},{2,3},{3,2},{4,5},{5,4},{6,7},{7,6}} | collective-permute-start | bytes 2654216 | tf_op jit(solution)/shard_map/ppermute | solution.py:288
  459.6 146.8 %collective-permute-start.35 = (bf16[4,144,768]{2,1,0:T(8,128)(2,1)}, bf16[4,144,768]{2,1,0:T(8,128)(2,1)}, u32[]{:S(2)}, u32[]{:S(2)}) collective-permute-start(bf16[4,144,768]{2,1,0:T(8,128)(2,1)} %get-tuple-element.81), channel_id=1, source_target_pairs={{0,2},{1,3},{2,0},{3,1},{4,6},{5,7},{6,4},{7,5}} | collective-permute-start | bytes 2654216 | tf_op jit(solution)/shard_map/ppermute | solution.py:288
  622.4 76.5 %collective-permute-start.29 = (f32[128,3072]{1,0:T(8,128)S(1)}, f32[128,3072]{1,0:T(8,128)}, u32[]{:S(2)}, u32[]{:S(2)}) collective-permute-start(f32[128,3072]{1,0:T(8,128)S(1)} %get-tuple-element.132), channel_id=1, source_target_pairs={{0,1},{1,0},{2,3},{3,2},{4,5},{5,4},{6,7},{7,6}} | collective-permute-start | bytes 4718600 | tf_op jit(solution)/shard_map/ppermute | solution.py:288
  702.2 79.8 %collective-permute-start.37 = (bf16[6,144,768]{2,1,0:T(8,128)(2,1)}, bf16[6,144,768]{2,1,0:T(8,128)(2,1)}, u32[]{:S(2)}, u32[]{:S(2)}) collective-permute-start(bf16[6,144,768]{2,1,0:T(8,128)(2,1)} %get-tuple-element.84), channel_id=1, source_target_pairs={{0,1},{1,0},{2,3},{3,2},{4,5},{5,4},{6,7},{7,6}} | collective-permute-start | bytes 3981320 | tf_op jit(solution)/shard_map/ppermute | solution.py:288
  702.5 81.0 %collective-permute-start.38 = (bf16[6,144,768]{2,1,0:T(8,128)(2,1)}, bf16[6,144,768]{2,1,0:T(8,128)(2,1)}, u32[]{:S(2)}, u32[]{:S(2)}) collective-permute-start(bf16[6,144,768]{2,1,0:T(8,128)(2,1)} %get-tuple-element.85), channel_id=1, source_target_pairs={{0,2},{1,3},{2,0},{3,1},{4,6},{5,7},{6,4},{7,5}} | collective-permute-start | bytes 3981320 | tf_op jit(solution)/shard_map/ppermute | solution.py:288
  703.0 81.0 %collective-permute-start.39 = (bf16[6,144,768]{2,1,0:T(8,128)(2,1)}, bf16[6,144,768]{2,1,0:T(8,128)(2,1)}, u32[]{:S(2)}, u32[]{:S(2)}) collective-permute-start(bf16[6,144,768]{2,1,0:T(8,128)(2,1)} %get-tuple-element.86), channel_id=1, source_target_pairs={{0,3},{1,2},{2,1},{3,0},{4,7},{5,6},{6,5},{7,4}} | collective-permute-start | bytes 3981320 | tf_op jit(solution)/shard_map/ppermute | solution.py:288
  704.4 81.1 %collective-permute-start.49 = (bf16[6,144,768]{2,1,0:T(8,128)(2,1)}, bf16[6,144,768]{2,1,0:T(8,128)(2,1)}, u32[]{:S(2)}, u32[]{:S(2)}) collective-permute-start(bf16[6,144,768]{2,1,0:T(8,128)(2,1)} %get-tuple-element.100), channel_id=1, source_target_pairs={{0,1},{1,0},{2,3},{3,2},{4,5},{5,4},{6,7},{7,6}} | collective-permute-start | bytes 3981320 | tf_op jit(solution)/shard_map/ppermute | solution.py:288
  706.7 74.8 %collective-permute-start.53 = (bf16[4,144,768]{2,1,0:T(8,128)(2,1)}, bf16[4,144,768]{2,1,0:T(8,128)(2,1)}, u32[]{:S(2)}, u32[]{:S(2)}) collective-permute-start(bf16[4,144,768]{2,1,0:T(8,128)(2,1)} %get-tuple-element.105), channel_id=1, source_target_pairs={{0,2},{1,3},{2,0},{3,1},{4,6},{5,7},{6,4},{7,5}} | collective-permute-start | bytes 2654216 | tf_op jit(solution)/shard_map/ppermute | solution.py:288
  783.5 88.2 %collective-permute-start.57 = (f32[128,3072]{1,0:T(8,128)}, f32[128,3072]{1,0:T(8,128)}, u32[]{:S(2)}, u32[]{:S(2)}) collective-permute-start(f32[128,3072]{1,0:T(8,128)} %get-tuple-element.108), channel_id=1, source_target_pairs={{0,2},{1,3},{2,0},{3,1},{4,6},{5,7},{6,4},{7,5}} | collective-permute-start | bytes 4718600 | tf_op jit(solution)/shard_map/ppermute | solution.py:288
  784.1 121.4 %collective-permute-start.59 = (f32[128,3072]{1,0:T(8,128)}, f32[128,3072]{1,0:T(8,128)}, u32[]{:S(2)}, u32[]{:S(2)}) collective-permute-start(f32[128,3072]{1,0:T(8,128)} %get-tuple-element.109), channel_id=1, source_target_pairs={{0,2},{1,3},{2,0},{3,1},{4,6},{5,7},{6,4},{7,5}} | collective-permute-start | bytes 4718600 | tf_op jit(solution)/shard_map/ppermute | solution.py:288
  785.5 153.6 %collective-permute-start.61 = (f32[128,3072]{1,0:T(8,128)}, f32[128,3072]{1,0:T(8,128)}, u32[]{:S(2)}, u32[]{:S(2)}) collective-permute-start(f32[128,3072]{1,0:T(8,128)} %get-tuple-element.110), channel_id=1, source_target_pairs={{0,2},{1,3},{2,0},{3,1},{4,6},{5,7},{6,4},{7,5}} | collective-permute-start | bytes 4718600 | tf_op jit(solution)/shard_map/ppermute | solution.py:288
  838.0 134.8 %collective-permute-start.63 = (f32[128,3072]{1,0:T(8,128)S(1)}, f32[128,3072]{1,0:T(8,128)}, u32[]{:S(2)}, u32[]{:S(2)}) collective-permute-start(f32[128,3072]{1,0:T(8,128)S(1)} %get-tuple-element.111), channel_id=1, source_target_pairs={{0,2},{1,3},{2,0},{3,1},{4,6},{5,7},{6,4},{7,5}} | collective-permute-start | bytes 4718600 | tf_op jit(solution)/shard_map/ppermute | solution.py:288
  838.6 168.0 %collective-permute-start.65 = (f32[128,3072]{1,0:T(8,128)S(1)}, f32[128,3072]{1,0:T(8,128)}, u32[]{:S(2)}, u32[]{:S(2)}) collective-permute-start(f32[128,3072]{1,0:T(8,128)S(1)} %get-tuple-element.112), channel_id=1, source_target_pairs={{0,2},{1,3},{2,0},{3,1},{4,6},{5,7},{6,4},{7,5}} | collective-permute-start | bytes 4718600 | tf_op jit(solution)/shard_map/ppermute | solution.py:288
  871.7 209.4 %collective-permute-start.68 = (f32[128,3072]{1,0:T(8,128)S(1)}, f32[128,3072]{1,0:T(8,128)S(1)}, u32[]{:S(2)}, u32[]{:S(2)}) collective-permute-start(f32[128,3072]{1,0:T(8,128)S(1)} %add.317.full_ref), channel_id=1, source_target_pairs={{0,1},{1,0},{2,3},{3,2},{4,5},{5,4},{6,7},{7,6}} | collective-permute-start | bytes 4718600 | tf_op jit(solution)/shard_map/ppermute | solution.py:288
  905.4 175.1 %collective-permute-start.50 = (bf16[6,144,768]{2,1,0:T(8,128)(2,1)S(1)}, bf16[6,144,768]{2,1,0:T(8,128)(2,1)S(1)}, u32[]{:S(2)}, u32[]{:S(2)}) collective-permute-start(bf16[6,144,768]{2,1,0:T(8,128)(2,1)S(1)} %copy-done.39), channel_id=1, source_target_pairs={{0,2},{1,3},{2,0},{3,1},{4,6},{5,7},{6,4},{7,5}} | collective-permute-start | bytes 3981320 | tf_op jit(solution)/shard_map/ppermute | solution.py:288
  939.1 141.4 %collective-permute-start.51 = (bf16[6,144,768]{2,1,0:T(8,128)(2,1)S(1)}, bf16[6,144,768]{2,1,0:T(8,128)(2,1)S(1)}, u32[]{:S(2)}, u32[]{:S(2)}) collective-permute-start(bf16[6,144,768]{2,1,0:T(8,128)(2,1)S(1)} %copy-done.38), channel_id=1, source_target_pairs={{0,3},{1,2},{2,1},{3,0},{4,7},{5,6},{6,5},{7,4}} | collective-permute-start | bytes 3981320 | tf_op jit(solution)/shard_map/ppermute | solution.py:288
  972.8 106.3 %collective-permute-start.54 = (bf16[4,144,768]{2,1,0:T(8,128)(2,1)S(1)}, bf16[4,144,768]{2,1,0:T(8,128)(2,1)S(1)}, u32[]{:S(2)}, u32[]{:S(2)}) collective-permute-start(bf16[4,144,768]{2,1,0:T(8,128)(2,1)S(1)} %copy-done.40), channel_id=1, source_target_pairs={{0,3},{1,2},{2,1},{3,0},{4,7},{5,6},{6,5},{7,4}} | collective-permute-start | bytes 2654216 | tf_op jit(solution)/shard_map/ppermute | solution.py:288
  1006.5 74.5 %collective-permute-start.56 = (f32[576,384]{1,0:T(8,128)S(1)}, f32[576,384]{1,0:T(8,128)S(1)}, u32[]{:S(2)}, u32[]{:S(2)}) collective-permute-start(f32[576,384]{1,0:T(8,128)S(1)} %add.311), channel_id=1, source_target_pairs={{0,1},{1,0},{2,3},{3,2},{4,5},{5,4},{6,7},{7,6}} | collective-permute-start | bytes 2654216 | tf_op jit(solution)/shard_map/ppermute | solution.py:288
  (82 other events, 3385.3 us)
